TPU v7x, 256 devices: a whole 4x4x8 slice. The times are simulated.
256 devices in a mesh: seq: 32 (over x, y, core), kvh: 8 (over z).
Axes of the slice: x: 4, y: 4, z: 8, core: 2. Of those that a mesh axis runs over, the one named last changes fastest.
Arguments:
- hidden: bfloat16 [24576, 4096], P('seq'), may hold values from -32 to 32
- w_query: bfloat16 [4096, 4096], P(None, 'kvh'), may hold values from -0.09375 to 0.09375
- w_key: bfloat16 [4096, 1024], P(None, 'kvh'), may hold values from -0.09375 to 0.09375
- w_value: bfloat16 [4096, 1024], P(None, 'kvh'), may hold values from -0.09375 to 0.09375
- cached_key: bfloat16 [24576, 1024], P('seq', 'kvh'), may hold values from -6 to 6
- cached_value: bfloat16 [24576, 1024], P('seq', 'kvh'), may hold values from -6 to 6
- doc_lengths: int32 [4], replicated, may hold values from 1 to 12288, 24576 in all
- selected: int32 [3840], replicated, may hold values from 0 to 767, as said below
Outputs:
- attended: bfloat16 [3840, 4096], P('seq', 'kvh')
- score: float32 [24576], P('seq')
Inputs may be any that keep to these rules, and one draw needn't show every extreme that they name: `selected`: each block of 120 entries holds distinct local row numbers in increasing order.
All inputs are finite; a program needn't handle non-finite values.
Results may differ from a plain program's by a relative error of at most 0.02.
Values may be sent and summed in bfloat16 or wider, within the bound.
No kernel may reach another device: no remote copies, remote signals or barrier semaphores. Data moves between devices by JAX's collectives and lax.ppermute only.
A program may use at most 192 MiB of HBM per device.

v0:
```python
import jax
import jax.numpy as jnp
from jax import lax
from jax.sharding import PartitionSpec as P

HEADS = 32
KV_HEADS = 8
HEAD_DIM = 128


def copy_for_each(shard, axis):
    copies = jnp.broadcast_to(shard, (lax.axis_size(axis), *shard.shape))
    return lax.all_to_all(copies, axis, split_axis=0, concat_axis=0, tiled=True)


def of_everyone(shard, axis):
    everything = copy_for_each(shard, axis)
    return jnp.sum(everything, axis=0)


def in_one_piece(arrays, axis, dim, along):
    widths = [a.shape[along] for a in arrays]
    both = jnp.concatenate(arrays, axis=along)
    result = lax.all_gather(both, axis, axis=dim, tiled=True)
    return tuple(jnp.split(result, [sum(widths[:k]) for k in range(1, len(widths))], axis=along))


def doc_numbers(positions, doc_lengths):
    boundary = jnp.cumsum(doc_lengths)
    return jnp.sum((positions[:, None] >= boundary[None, :]).astype(jnp.int32), axis=1)


def shards(hidden, w_query, w_key, w_value, cached_key, cached_value, doc_lengths, selected):
    tok_rows = hidden.shape[0]
    seq_count = lax.axis_size("seq")
    seq_place = lax.axis_index("seq")
    sel_rows = selected.shape[0] // seq_count
    local_heads = w_key.shape[1] // HEAD_DIM
    group_size = HEADS // KV_HEADS
    scaling = HEAD_DIM ** (-0.5)
    doc_count = doc_lengths.shape[0]
    key_fresh = jnp.dot(hidden, w_key, preferred_element_type=jnp.float32)
    value_fresh = jnp.dot(hidden, w_value, preferred_element_type=jnp.float32)
    key_shift = key_fresh - cached_key.astype(jnp.float32)
    value_shift = value_fresh - cached_value.astype(jnp.float32)
    head_dev = jnp.sum(key_shift * key_shift, axis=1) + jnp.sum(value_shift * value_shift, axis=1)
    first_row = seq_place * tok_rows
    positions = first_row + jnp.arange(tok_rows, dtype=jnp.int32)
    doc_of = doc_numbers(positions, doc_lengths)
    doc_table = (doc_of[:, None] == jnp.arange(doc_count, dtype=jnp.int32)[None, :]).astype(
        jnp.float32
    )
    deviation = of_everyone(head_dev, "kvh")
    doc_part = jnp.dot(deviation, doc_table)
    doc_total = of_everyone(doc_part, "seq")
    doc_mean = doc_total / doc_lengths.astype(jnp.float32)
    score = deviation / (jnp.dot(doc_table, doc_mean) + 1.0)
    own_rows = lax.dynamic_slice_in_dim(selected, seq_place * sel_rows, sel_rows, 0)
    chosen = jnp.any(own_rows[:, None] == jnp.arange(tok_rows, dtype=jnp.int32)[None, :], axis=0)
    key_used = jnp.where(chosen[:, None], key_fresh.astype(jnp.bfloat16), cached_key)
    value_used = jnp.where(chosen[:, None], value_fresh.astype(jnp.bfloat16), cached_value)
    picked_states = jnp.take(hidden, own_rows, axis=0)
    queries = jnp.dot(picked_states, w_query, preferred_element_type=jnp.float32).astype(
        jnp.bfloat16
    )
    query_pos = first_row + own_rows
    query_split = queries.reshape(sel_rows, local_heads, group_size, HEAD_DIM)
    start_max = jnp.full((sel_rows, local_heads, group_size), -1e30, jnp.float32)
    keys_here, values_here = in_one_piece((key_used, value_used), "seq", 0, 1)
    piece_rows = keys_here.shape[0]
    key_pos = jnp.arange(piece_rows, dtype=jnp.int32)
    allowed = key_pos[None, :] <= query_pos[:, None]
    keep = allowed[:, None, None, :]
    key_split = keys_here.reshape(piece_rows, local_heads, HEAD_DIM)
    value_split = values_here.reshape(piece_rows, local_heads, HEAD_DIM)
    scores = (
        jnp.einsum("sagd,nad->sagn", query_split, key_split, preferred_element_type=jnp.float32)
        * scaling
    )
    scores = jnp.where(keep, scores, -1e30)
    new_max = jnp.maximum(start_max, jnp.max(scores, axis=3))
    weights = jnp.where(keep, jnp.exp(scores - new_max[..., None]), 0.0)
    row_sum = jnp.sum(weights, axis=3)
    mixed = jnp.einsum(
        "sagn,nad->sagd",
        weights.astype(jnp.bfloat16),
        value_split,
        preferred_element_type=jnp.float32,
    )
    final_max, row_sum, mixed = (new_max, row_sum, mixed)
    attended = (
        (mixed / row_sum[..., None])
        .reshape(sel_rows, local_heads * group_size * HEAD_DIM)
        .astype(jnp.bfloat16)
    )
    return (attended, score)


def solution(mesh):
    return jax.shard_map(
        shards,
        mesh=mesh,
        in_specs=(
            P("seq", None),
            P(None, "kvh"),
            P(None, "kvh"),
            P(None, "kvh"),
            P("seq", "kvh"),
            P("seq", "kvh"),
            P(),
            P(),
        ),
        out_specs=(P("seq", "kvh"), P("seq")),
        check_vma=False,
    )
```

profile of v0, /device:TPU:1, one launch (start us, length us, event | category | flops | bytes accessed | tf_op | source)
XLA Modules:
  0.0 163.6 jit_solution(3078265807513575370)
XLA Ops:
  7.2 0.0 copy-start
  7.2 0.0 slice-start
  7.2 0.0 all-gather.2.cloned.1.call-start
  7.2 0.9 broadcast_add_fusion
  8.2 0.1 fusion.24
  8.3 1.1 copy.33
  9.4 1.1 copy.34
  10.4 0.0 slice-start.1
  10.5 5.4 %multiply_reduce_fusion = (f32[768]{0:T(1024)S(1)}, bf16[768,128]{0,1:T(8,128)(2,1)S(1)}) fusion(bf16[768,128]{0,1:T(8,128)(2,1)S(1)} %copy.34, bf16[768,4096]{1,0:T(8,128)(2,1)} %param.8, bf16[4096,128]{1,0:T(8,128)(2,1)} %param.11), kind=kOutput, calls=%fused_computation.26 | convolution fusion | flops 805797120 | bytes 7736320 | tf_op jit(solution)/shard_map/dot_general | solution.py:43
  15.9 3.0 %convert_select_fusion.1 = (bf16[768,128]{0,1:T(8,128)(2,1)S(1)}, bf16[768,128]{0,1:T(8,128)(2,1)S(1)}, f32[768,128]{0,1:T(8,128)}) fusion(bf16[768,128]{0,1:T(8,128)(2,1)S(1)} %copy.33, pred[768]{0:T(1024)(128)(4,1)S(1)} %fusion.24, bf16[768,128]{0,1:T(8,128)(2,1)S(1)} %copy.34, bf16[768,128]{0,1:T(8,128)(2,1)S(1)} %get-tuple-element.10, ...), kind=kOutput, calls=%fused_computation.33 | convolution fusion | flops 805601280 | bytes 8717056 | tf_op jit(solution)/shard_map/dot_general | solution.py:42
  18.9 0.8 pad_maximum_fusion
  19.7 0.0 all-gather.2.cloned.1.call-update
  19.7 1.1 multiply_reduce_fusion.1
  20.8 0.6 broadcast_in_dim.71
  21.4 9.0 %all-to-all-start = ((f32[8,1,768]{2,1,0:T(1,128)}), f32[8,1,768]{2,1,0:T(1,128)S(1)}, u32[]{:S(2)}, u32[]{:S(2)}) async-start(f32[8,1,768]{2,1,0:T(1,128)} %broadcast_in_dim.71), calls=%async_computation | async-start | bytes 49152 | tf_op jit(solution)/shard_map/all_to_all | solution.py:13
  30.4 0.8 reduce-window.8
  31.2 0.1 convert_reduce_fusion
  31.3 3.3 %iota_compare_fusion = pred[120,24576]{1,0:T(8,128)(4,1)} fusion(s32[120]{0:T(128)S(1)} %get-tuple-element.2), kind=kLoop, calls=%fused_computation.9 | loop fusion | flops 2949120 | bytes 2949600 | tf_op jit(solution)/shard_map/le | solution.py:72
  34.7 6.0 %gather_fusion = bf16[120,4096]{1,0:T(8,128)(2,1)S(1)} fusion(bf16[768,4096]{1,0:T(8,128)(2,1)} %param.8, s32[1024]{0:T(1024)S(1)} %pad_clamp_fusion), kind=kCustom, calls=%fused_computation | custom fusion | bytes 1966560 | tf_op jit(solution)/shard_map/jit(_take)/gather | solution.py:62
  40.7 0.3 convolution_bitcast_fusion
  41.0 0.6 broadcast_in_dim.72
  41.6 8.1 %all-to-all-start.1 = ((f32[32,1,4]{2,1,0:T(1,128)}), f32[32,1,4]{2,1,0:T(1,128)S(1)}, u32[]{:S(2)}, u32[]{:S(2)}) async-start(f32[32,1,4]{2,1,0:T(1,128)} %broadcast_in_dim.72), calls=%async_computation.1 | async-start | bytes 32768 | tf_op jit(solution)/shard_map/all_to_all | solution.py:13
  49.7 3.0 %fusion.11 = bf16[15,4,8,128]{3,2,1,0:T(8,128)(2,1)S(1)} fusion(bf16[4096,512]{1,0:T(8,128)(2,1)} %param.9, bf16[120,4096]{1,0:T(8,128)(2,1)S(1)} %gather_fusion, pred[120]{0:T(512)(128)(4,1)S(1)} %compare_and_fusion), kind=kOutput, calls=%fused_computation.15 | convolution fusion | flops 503869440 | bytes 5300344 | tf_op jit(solution)/shard_map/dot_general | solution.py:63
  52.7 3.9 %all-to-all-done.1 = f32[32,1,4]{2,1,0:T(1,128)S(1)} async-done(((f32[32,1,4]{2,1,0:T(1,128)}), f32[32,1,4]{2,1,0:T(1,128)S(1)}, u32[]{:S(2)}, u32[]{:S(2)}) %all-to-all-start.1) | async-done | bytes 544 | tf_op jit(solution)/shard_map/all_to_all | solution.py:13
  56.6 0.1 reduce_sum.59
  56.6 0.3 convolution_reduce_fusion
  56.9 0.6 add_divide_fusion
  57.5 34.0 %all-gather.2.cloned.1.call-done = bf16[24576,256]{0,1:T(8,128)(2,1)} async-done(((bf16[768,256]{0,1:T(8,128)(2,1)}), bf16[24576,256]{0,1:T(8,128)(2,1)}) %all-gather.2.cloned.1.call-update) | async-done | bytes 12582928 | tf_op jit(solution)/shard_map/all_gather | solution.py:24
  91.5 20.6 %fusion = (f32[120,4]{0,1:T(4,128)S(1)}, f32[24576,120,4]{0,1,2:T(8,128)}) fusion(pred[120,24576]{1,0:T(8,128)(4,1)} %iota_compare_fusion, bf16[15,4,8,128]{3,2,1,0:T(8,128)(2,1)S(1)} %fusion.11, bf16[24576,256]{0,1:T(8,128)(2,1)} %all-gather.2.cloned.1.call-done), kind=kOutput, calls=%fused_computation.3 | convolution fusion | flops 3055287808 | bytes 56551296 | tf_op jit(solution)/shard_map/sagd,nad->sagn/dot_general | solution.py:77
  112.2 21.9 %fusion.1 = f32[120,4]{0,1:T(4,128)S(1)} fusion(f32[24576,120,4]{0,1,2:T(8,128)} %get-tuple-element.8, f32[120,4]{0,1:T(4,128)S(1)} %broadcast_maximum_fusion, pred[120,24576]{1,0:T(8,128)(4,1)} %iota_compare_fusion), kind=kLoop, calls=%fused_computation.4 | loop fusion | flops 58981920 | bytes 50138880 | tf_op jit(solution)/shard_map/reduce_sum | solution.py:83
  134.1 21.9 %fusion.18 = bf16[120,1,4,128]{3,0,2,1:T(8,128)(2,1)S(1)} fusion(f32[24576,120,4]{0,1,2:T(8,128)} %get-tuple-element.8, f32[120,4]{0,1:T(4,128)S(1)} %broadcast_maximum_fusion, pred[120,24576]{1,0:T(8,128)(4,1)} %iota_compare_fusion, bf16[24576,256]{0,1:T(8,128)(2,1)} %all-gather.2.cloned.1.call-done, f32[120,4]{0,1:T(4,128)S(1)} %fusion.1), kind=kOutput, calls=%fused_computation.20 | convolution fusion | flops 3079004160 | bytes 56553216 | tf_op jit(solution)/shard_map/sagn,nad->sagd/dot_general | solution.py:84
  156.1 0.7 copy.58
  (18 shorter events, 0.1 us)
Async XLA Ops:
  7.2 8.7 %copy-start = (bf16[4096,128]{1,0:T(8,128)(2,1)S(1)}, bf16[4096,128]{1,0:T(8,128)(2,1)}, u32[]{:S(2)}) copy-start(bf16[4096,128]{1,0:T(8,128)(2,1)} %param.10) | copy-start | bytes 3145732
  7.2 8.7 %slice-start = ((s8[6291456]{0:T(1024)(128)(4,1)}), s8[2097152]{0:T(1024)(128)(4,1)S(1)}, s32[]{:S(2)}) async-start(s8[6291456]{0:T(1024)(128)(4,1)} %bitcast.86), calls=%async_computation.3 | async-start | bytes 4194304
  7.2 84.3 %all-gather.2.cloned.1.call-start = ((), (), s32[]{:S(2)}) async-start(), calls=%async_computation.2 | async-start | bytes 12976128 | tf_op jit(solution)/shard_map/all_gather | solution.py:24
  10.4 5.5 %slice-start.1 = ((s8[6291456]{0:T(1024)(128)(4,1)}), s8[4194304]{0:T(1024)(128)(4,1)S(1)}, s32[]{:S(2)}) async-start(s8[6291456]{0:T(1024)(128)(4,1)} %bitcast.86), calls=%async_computation.4 | async-start | bytes 8388608
  18.9 37.7 %copy-start.2 = (s32[4]{0:T(128)S(1)}, s32[4]{0:T(128)}, u32[]{:S(2)}) copy-start(s32[4]{0:T(128)} %param.14) | copy-start | bytes 52
  21.4 19.3 %all-to-all-start = ((f32[8,1,768]{2,1,0:T(1,128)}), f32[8,1,768]{2,1,0:T(1,128)S(1)}, u32[]{:S(2)}, u32[]{:S(2)}) async-start(f32[8,1,768]{2,1,0:T(1,128)} %broadcast_in_dim.71), calls=%async_computation | async-start | bytes 49152 | tf_op jit(solution)/shard_map/all_to_all | solution.py:13
  41.6 15.0 %all-to-all-start.1 = ((f32[32,1,4]{2,1,0:T(1,128)}), f32[32,1,4]{2,1,0:T(1,128)S(1)}, u32[]{:S(2)}, u32[]{:S(2)}) async-start(f32[32,1,4]{2,1,0:T(1,128)} %broadcast_in_dim.72), calls=%async_computation.1 | async-start | bytes 32768 | tf_op jit(solution)/shard_map/all_to_all | solution.py:13
  134.1 22.7 %copy-start.1 = (bf16[4096,128]{1,0:T(8,128)(2,1)S(1)}, bf16[4096,128]{1,0:T(8,128)(2,1)}, u32[]{:S(2)}) copy-start(bf16[4096,128]{1,0:T(8,128)(2,1)} %param.10) | copy-start | bytes 3145732
Sparse Core Ops, SparseCore 0:
  19.8 71.6 all-gather.1
where the time goes:
time: 164 us
  matrix products  54.5 us (33%)
  waiting for transfers between devices  37.9 us (23%)
  other arithmetic  29.8 us (18%)
  starting transfers between devices  17.1 us (10%)
  between operations  14.2 us (9%)
  local copies, waits for them, and re-layouts  10.1 us (6%)
    all_gather x1, waiting for transfers between devices, in_one_piece(): result = lax.all_gather(both, axis, axis=dim, tiled=True)  34 us
    reduce_sum x1, other arithmetic, shards(): row_sum = jnp.sum(weights, axis=3)  21.9 us
    dot_general x1, matrix products, shards(): jnp.einsum('sagn,nad->sagd', weights.astype(jnp.bfloat16), value_split, p...  21.9 us
    dot_general x1, matrix products, shards(): jnp.einsum('sagd,nad->sagn', query_split, key_split, preferred_element_ty...  20.6 us
    all_to_all x2, starting transfers between devices, copy_for_each(): return lax.all_to_all(copies, axis, split_axis=0, concat_axis=0, tiled=True)  17.1 us
    gather x1, local copies, waits for them, and re-layouts, shards(): picked_states = jnp.take(hidden, own_rows, axis=0)  5.97 us
    dot_general x1, matrix products, shards(): value_fresh = jnp.dot(hidden, w_value, preferred_element_type=jnp.float32)  5.42 us
    all_to_all x2, waiting for transfers between devices, copy_for_each(): return lax.all_to_all(copies, axis, split_axis=0, concat_axis=0, tiled=True)  3.92 us
  transfers between devices with their start and end apart: 3, of which 2 were waited for; matrix products, arithmetic and copies ran while one was open for 10% of the time, Pallas kernels for 0%

commit v1 on v0

v1 whole, which is shorter than its diff:
```python
import functools
import math

import jax
import jax.numpy as jnp
from jax import lax
from jax.experimental import pallas as pl
from jax.experimental.pallas import tpu as pltpu
from jax.sharding import Mesh, PartitionSpec as P

HEADS = 32
KV_HEADS = 8
HEAD_DIM = 128
GROUP = 4
TOK = 768
SEL = 120
ROWS = 128
QROWS = GROUP * ROWS
DOCS = 4
CHUNK = 512
NEG = -1e30
EXP_SCALE = (HEAD_DIM ** -0.5) * math.log2(math.e)
SEQ = ("x", "y", "c")
f32, bf16 = jnp.float32, jnp.bfloat16


def seq_number():
    return (lax.axis_index("x") * 4 + lax.axis_index("y")) * 2 + lax.axis_index("c")


def doc_ends(lengths):
    ends = [lengths[0]]
    for d in range(1, DOCS):
        ends.append(ends[-1] + lengths[d])
    return ends


def project_kernel(lengths, own, hidden, w_query, w_key, w_value, cached_key, cached_value,
                   kv_out, q_out, dev_out, pick, acc_kv, acc_q):
    step = pl.program_id(0)

    @pl.when(step == 0)
    def _():
        across = jnp.broadcast_to(own[...], (ROWS, ROWS)).astype(f32).T
        tokens = lax.broadcasted_iota(jnp.int32, (ROWS, TOK), 1).astype(f32)
        wide = jnp.concatenate([across] * (TOK // ROWS), axis=1)
        pick[...] = jnp.where(wide == tokens, 1.0, 0.0).astype(bf16)
        acc_kv[...] = jnp.zeros_like(acc_kv)
        acc_q[...] = jnp.zeros_like(acc_q)

    states = hidden[...]
    both = jnp.concatenate([w_key[...], w_value[...]], axis=1)
    acc_kv[...] += jnp.dot(states, both, preferred_element_type=f32)
    picked = jnp.dot(pick[...], states, preferred_element_type=f32).astype(bf16)
    acc_q[...] += jnp.dot(picked, w_query[...], preferred_element_type=f32)

    @pl.when(step == pl.num_programs(0) - 1)
    def _():
        tokens = lax.broadcasted_iota(jnp.int32, (TOK, ROWS), 0)
        hit = jnp.where(tokens == own[...], 1.0, 0.0)
        chosen = jnp.max(hit, axis=1, keepdims=True) > 0.0
        old_key = cached_key[...].astype(f32)
        old_value = cached_value[...].astype(f32)
        new_key = acc_kv[:, :HEAD_DIM]
        new_value = acc_kv[:, HEAD_DIM:]
        kv_out[:TOK, :] = jnp.where(chosen, new_key, old_key).astype(bf16)
        value_used = jnp.where(chosen, new_value, old_value)
        for t in range(TOK // ROWS):
            kv_out[TOK + t * ROWS:TOK + (t + 1) * ROWS, :] = (
                value_used[t * ROWS:(t + 1) * ROWS, :].T.astype(bf16))
        for h in range(GROUP):
            q_out[h * ROWS:(h + 1) * ROWS, :] = acc_q[:, h * HEAD_DIM:(h + 1) * HEAD_DIM].astype(bf16)
        shift = (new_key - old_key) ** 2 + (new_value - old_value) ** 2
        first = seq_number() * TOK
        ends = doc_ends(lengths)
        lane = lax.broadcasted_iota(jnp.int32, (1, ROWS), 1)
        totals = [jnp.zeros((1, ROWS), f32) for _ in range(DOCS)]
        for t in range(TOK // ROWS):
            dev = jnp.sum(shift[t * ROWS:(t + 1) * ROWS, :].T, axis=0, keepdims=True)
            dev_out[t:t + 1, :] = dev
            place = lane + (first + t * ROWS)
            doc = sum([(place >= e).astype(jnp.int32) for e in ends])
            for d in range(DOCS):
                totals[d] = totals[d] + jnp.where(doc == d, dev, 0.0)
        row = jnp.zeros((1, ROWS), f32)
        for d in range(DOCS):
            row = jnp.where(lane == d, jnp.sum(totals[d], axis=1, keepdims=True), row)
        dev_out[6:7, :] = row
        dev_out[7:8, :] = jnp.zeros((1, ROWS), f32)


def project(lengths, own, hidden, w_query, w_key, w_value, cached_key, cached_value):
    steps = hidden.shape[1] // CHUNK
    whole = lambda k: (0, 0)
    return pl.pallas_call(
        project_kernel,
        grid=(steps,),
        in_specs=[
            pl.BlockSpec(memory_space=pltpu.SMEM),
            pl.BlockSpec((1, ROWS), whole),
            pl.BlockSpec((TOK, CHUNK), lambda k: (0, k)),
            pl.BlockSpec((CHUNK, GROUP * HEAD_DIM), lambda k: (k, 0)),
            pl.BlockSpec((CHUNK, HEAD_DIM), lambda k: (k, 0)),
            pl.BlockSpec((CHUNK, HEAD_DIM), lambda k: (k, 0)),
            pl.BlockSpec((TOK, HEAD_DIM), whole),
            pl.BlockSpec((TOK, HEAD_DIM), whole),
        ],
        out_specs=[
            pl.BlockSpec((2 * TOK, HEAD_DIM), whole),
            pl.BlockSpec((QROWS, HEAD_DIM), whole),
            pl.BlockSpec((8, ROWS), whole),
        ],
        out_shape=[
            jax.ShapeDtypeStruct((2 * TOK, HEAD_DIM), bf16),
            jax.ShapeDtypeStruct((QROWS, HEAD_DIM), bf16),
            jax.ShapeDtypeStruct((8, ROWS), f32),
        ],
        scratch_shapes=[
            pltpu.VMEM((ROWS, TOK), bf16),
            pltpu.VMEM((TOK, 2 * HEAD_DIM), f32),
            pltpu.VMEM((ROWS, GROUP * HEAD_DIM), f32),
        ],
        compiler_params=pltpu.CompilerParams(vmem_limit_bytes=24 * 2**20),
        cost_estimate=pl.CostEstimate(flops=2 * 10**9, bytes_accessed=13 * 10**6, transcendentals=0),
        name="project",
    )(lengths, own, hidden, w_query, w_key, w_value, cached_key, cached_value)


X_STEPS = (0, 1, 3, 2)
Y_STEPS = (0, 1, 3, 2)
QT = 256


def attend_pair(q, kv, m_s, l_s, acc_s, i, j, mask_rows):
    keys = kv[j, :TOK, :]
    for t in range(QROWS // QT):
        cols = slice(t * QT, (t + 1) * QT)
        s = lax.dot_general(keys, q[i, cols, :], (((1,), (1,)), ((), ())), preferred_element_type=f32)
        if mask_rows is not None:
            place = lax.broadcasted_iota(jnp.int32, (TOK, QT), 0)
            s = jnp.where(place <= mask_rows[:, cols], s, NEG)
        old = m_s[i, 0:1, cols]
        new = jnp.maximum(old, jnp.max(s, axis=0, keepdims=True))
        p = jnp.exp2((s - new) * EXP_SCALE)
        fade = jnp.exp2((old - new) * EXP_SCALE)
        m_s[i, 0:1, cols] = new
        l_s[i, 0:1, cols] = l_s[i, 0:1, cols] * fade + jnp.sum(p, axis=0, keepdims=True)
        pb = p.astype(bf16)
        mixed = acc_s[i, :, cols] * fade
        values = jnp.concatenate(
            [kv[j, TOK + k * ROWS:TOK + (k + 1) * ROWS, :] for k in range(TOK // ROWS)], axis=1)
        acc_s[i, :, cols] = mixed + jnp.dot(values, pb, preferred_element_type=f32)


def attend_kernel(mask_rows, *refs):
    q_in, kv_in, outs = refs[:4], refs[4:12], refs[12:16]
    q, kv, m_s, l_s, acc_s, q_sem, kv_sem = refs[16:]
    q_copies = [pltpu.make_async_copy(q_in[i], q.at[i], q_sem.at[i]) for i in range(4)]
    kv_copies = [pltpu.make_async_copy(kv_in[j], kv.at[j], kv_sem.at[j]) for j in range(8)]
    q_copies[0].start()
    kv_copies[0].start()
    for c in q_copies[1:] + kv_copies[1:]:
        c.start()
    m_s[...] = jnp.full_like(m_s, NEG)
    l_s[...] = jnp.zeros_like(l_s)
    acc_s[...] = jnp.zeros_like(acc_s)
    x, y, c = lax.axis_index("x"), lax.axis_index("y"), lax.axis_index("c")
    for copy in q_copies:
        copy.wait()
    kv_copies[0].wait()
    attend_pair(q, kv, m_s, l_s, acc_s, 0, 0, mask_rows)
    for copy in kv_copies[1:]:
        copy.wait()

    @pl.loop(0, 32)
    def _(n):
        i = n // 8
        j = n % 8
        dx = jnp.where(i == 2, 3, jnp.where(i == 3, 2, i))
        k = j // 2
        dy = jnp.where(k == 2, 3, jnp.where(k == 3, 2, k))
        q_at = ((x + dx) % 4) * 8 + 2 * y + c
        kv_at = x * 8 + 2 * ((y + dy) % 4) + (c + j % 2) % 2

        @pl.when(q_at > kv_at)
        def _():
            attend_pair(q, kv, m_s, l_s, acc_s, i, j, None)

    for i in range(4):
        total = l_s[i, 0:1, :]
        outs[i][:HEAD_DIM, :] = (acc_s[i] / jnp.maximum(total, 1e-30)).astype(bf16)
        lse = jnp.where(total > 0.0, m_s[i, 0:1, :] * EXP_SCALE + jnp.log2(jnp.maximum(total, 1e-30)), NEG)
        high = lse.astype(bf16)
        rest = lse - high.astype(f32)
        mid = rest.astype(bf16)
        low = (rest - mid.astype(f32)).astype(bf16)
        outs[i][HEAD_DIM:, :] = jnp.concatenate(
            [high.astype(f32), mid.astype(f32), low.astype(f32), jnp.zeros((13, QROWS), f32)], axis=0).astype(bf16)


def attend(mask_rows, qs, kvs):
    hbm = pl.BlockSpec(memory_space=pltpu.HBM)
    vmem = pl.BlockSpec(memory_space=pltpu.VMEM)
    return pl.pallas_call(
        attend_kernel,
        in_specs=[vmem] + [hbm] * 12,
        out_specs=[vmem] * 4,
        out_shape=[jax.ShapeDtypeStruct((HEAD_DIM + 16, QROWS), bf16)] * 4,
        scratch_shapes=[
            pltpu.VMEM((4, QROWS, HEAD_DIM), bf16),
            pltpu.VMEM((8, 2 * TOK, HEAD_DIM), bf16),
            pltpu.VMEM((4, 8, QROWS), f32),
            pltpu.VMEM((4, 8, QROWS), f32),
            pltpu.VMEM((4, HEAD_DIM, QROWS), f32),
            pltpu.SemaphoreType.DMA((4,)),
            pltpu.SemaphoreType.DMA((8,)),
        ],
        compiler_params=pltpu.CompilerParams(vmem_limit_bytes=40 * 2**20),
        cost_estimate=pl.CostEstimate(flops=12 * 10**9, bytes_accessed=4 * 10**6, transcendentals=12 * 10**6),
        name="attend",
    )(mask_rows, *qs, *kvs)


def combine_kernel(lengths, dev, p0, p1, p2, p3, out, score):
    parts = (p0, p1, p2, p3)
    lses = [p[HEAD_DIM:HEAD_DIM + 16, :].astype(f32) for p in parts]
    lses = [v[0:1] + v[1:2] + v[2:3] for v in lses]
    top = functools.reduce(jnp.maximum, lses)
    weights = [jnp.exp2(v - top) for v in lses]
    scale = 1.0 / sum(weights)
    mixed = sum([p[:HEAD_DIM, :].astype(f32) * (w * scale) for p, w in zip(parts, weights)])
    for h in range(GROUP):
        out[:, h * HEAD_DIM:(h + 1) * HEAD_DIM] = (
            mixed[:, h * ROWS:(h + 1) * ROWS].T[:SEL, :].astype(bf16))
    first = seq_number() * TOK
    ends = doc_ends(lengths)
    lane = lax.broadcasted_iota(jnp.int32, (8, ROWS), 1)
    place = lane + lax.broadcasted_iota(jnp.int32, (8, ROWS), 0) * ROWS + first
    doc = sum([(place >= e).astype(jnp.int32) for e in ends])
    mean = jnp.zeros((8, ROWS), f32)
    for d in range(DOCS):
        mean = jnp.where(doc == d, dev[6:7, d:d + 1] / lengths[d].astype(f32), mean)
    score[...] = dev[...] / (mean + 1.0)


def combine(lengths, dev, parts):
    vmem = pl.BlockSpec(memory_space=pltpu.VMEM)
    return pl.pallas_call(
        combine_kernel,
        in_specs=[pl.BlockSpec(memory_space=pltpu.SMEM)] + [vmem] * 5,
        out_specs=[vmem, vmem],
        out_shape=[
            jax.ShapeDtypeStruct((SEL, GROUP * HEAD_DIM), bf16),
            jax.ShapeDtypeStruct((8, ROWS), f32),
        ],
        compiler_params=pltpu.CompilerParams(vmem_limit_bytes=8 * 2**20),
        cost_estimate=pl.CostEstimate(flops=10**6, bytes_accessed=10**6, transcendentals=0),
        name="combine",
    )(lengths, dev, *parts)


def fetch(value, axis, step):
    size = lax.axis_size(axis)
    return lax.ppermute(value, axis, [((i + step) % size, i) for i in range(size)])


def exchange(value, axis, bit):
    size = lax.axis_size(axis)
    return lax.ppermute(value, axis, [(i, i ^ bit) for i in range(size)])


def shards(hidden, w_query, w_key, w_value, cached_key, cached_value, doc_lengths, selected):
    own = lax.dynamic_slice_in_dim(selected, seq_number() * SEL, SEL, 0)
    rows = jnp.pad(own, (0, ROWS - SEL), constant_values=-1)[None, :]
    mask_rows = jnp.tile(jnp.pad(own, (0, ROWS - SEL), constant_values=TOK)[None, :], (1, GROUP))
    kv, q, dev = project(doc_lengths, rows, hidden, w_query, w_key, w_value, cached_key, cached_value)
    kv_y = [kv] + [fetch(kv, "y", s) for s in Y_STEPS[1:]]
    qs = [q] + [fetch(q, "x", s) for s in X_STEPS[1:]]
    kvs = []
    for block in kv_y:
        kvs += [block, exchange(block, "c", 1)]
    for bit in (1, 2, 4):
        dev = dev + exchange(dev, "kvh", bit)
    docs = dev
    for axis, bit in (("c", 1), ("y", 1), ("y", 2), ("x", 1), ("x", 2)):
        docs = docs + exchange(docs, axis, bit)
    dev = jnp.concatenate([dev[:6], docs[6:]], axis=0)
    parts = attend(mask_rows, qs, kvs)
    mine = [parts[0]]
    for n, s in enumerate(X_STEPS[1:]):
        back = (4 - s) % 4
        mine.append(fetch(parts[n + 1], "x", back))
    attended, score = combine(doc_lengths, dev, mine)
    return attended, score.reshape(-1)[:TOK]


def solution(mesh):
    fine = Mesh(mesh.devices.reshape(4, 4, 2, 8), ("x", "y", "c", "kvh"))
    return jax.shard_map(
        shards,
        mesh=fine,
        in_specs=(
            P(SEQ, None),
            P(None, "kvh"),
            P(None, "kvh"),
            P(None, "kvh"),
            P(SEQ, "kvh"),
            P(SEQ, "kvh"),
            P(),
            P(),
        ),
        out_specs=(P(SEQ, "kvh"), P(SEQ)),
        check_vma=False,
    )
```

time: 164 us -> 133 us (0.81)
  the two profiles are of different devices: /device:TPU:1 before, /device:TPU:28 now
where the time goes in v1:
time: 133 us
  waiting for transfers between devices  49.5 us (37%)
  starting transfers between devices  41.9 us (32%)
  Pallas kernels  29.5 us (22%)
  local copies, waits for them, and re-layouts  11.3 us (8%)
    ppermute x9, starting transfers between devices, fetch(): lax.ppermute(value, axis, [((i + step) % size, i) for i in range(size)])  29.8 us
    ppermute x9, waiting for transfers between devices, fetch(): lax.ppermute(value, axis, [((i + step) % size, i) for i in range(size)])  26 us
    ppermute x12, waiting for transfers between devices, exchange(): return lax.ppermute(value, axis, [(i, i ^ bit) for i in range(size)])  23.4 us
    pallas_call x1, Pallas kernels, attend(): pl.pallas_call(attend_kernel, in_specs=[vmem] + [hbm] * 12, out_specs=[vm...  21.5 us
    ppermute x12, starting transfers between devices, exchange(): return lax.ppermute(value, axis, [(i, i ^ bit) for i in range(size)])  12.1 us
    unnamed x16, local copies, waits for them, and re-layouts  9.93 us
    pallas_call x1, Pallas kernels, project(): pl.pallas_call(project_kernel, grid=(steps,), in_specs=[pl.BlockSpec(memo...  6.52 us
  transfers between devices with their start and end apart: 21, of which 13 were waited for; matrix products, arithmetic and copies ran while one was open for 0% of the time, Pallas kernels for 0%

profile of v1, /device:TPU:28, one launch (start us, length us, event | category | flops | bytes accessed | tf_op | source)
XLA Modules:
  0.0 132.9 jit_solution(9673120677817023963)
XLA Ops:
  0.6 0.8 dynamic_slice.3
  1.4 2.8 %copy-done = bf16[768,4096]{1,0:T(8,128)(2,1)S(1)} copy-done((bf16[768,4096]{1,0:T(8,128)(2,1)S(1)}, bf16[768,4096]{1,0:T(8,128)(2,1)}, u32[]{:S(2)}) %copy-start) | copy-done | bytes 6291480
  4.2 2.2 %copy-done.1 = bf16[4096,512]{1,0:T(8,128)(2,1)S(1)} copy-done((bf16[4096,512]{1,0:T(8,128)(2,1)S(1)}, bf16[4096,512]{1,0:T(8,128)(2,1)}, u32[]{:S(2)}) %copy-start.1) | copy-done | bytes 4194328
  6.4 1.2 copy-done.2
  7.6 1.2 copy-done.3
  8.8 0.9 copy-done.4
  9.8 0.9 copy-done.5
  10.7 0.7 copy-done.6
  11.4 6.5 %project.1 = (bf16[1536,128]{1,0:T(8,128)(2,1)S(1)}, bf16[512,128]{1,0:T(8,128)(2,1)S(1)}, f32[8,128]{1,0:T(8,128)S(1)}) custom-call(s32[4]{0:T(128)S(1)} %copy-done.6, s32[1,128]{1,0:T(1,128)S(1)} %get-tuple-element.21.own, bf16[768,4096]{1,0:T(8,128)(2,1)S(1)} %copy-done, bf16[4096,512]{1,0:T(8,128)(2,1)S(1)} %copy-done.1, ...), custom_call_target="tpu_custom_call" | custom-call | flops 2000000000 | bytes 13000000 | tf_op jit(solution)/shard_map/project/pallas_call | solution.py:95
  17.9 1.3 collective-permute-start.16
  19.2 2.2 %collective-permute-start.14 = (bf16[1536,128]{1,0:T(8,128)(2,1)S(1)}, bf16[1536,128]{1,0:T(8,128)(2,1)S(1)}, u32[]{:S(2)}, u32[]{:S(2)}) collective-permute-start(bf16[1536,128]{1,0:T(8,128)(2,1)S(1)} %get-tuple-element.13.refs_4_), channel_id=1, source_target_pairs={{48,0},{0,16},{16,32},{32,48},{49,1},{1,17},{17,33},{33,49},{50,2}... | collective-permute-start | bytes 1179656 | tf_op jit(solution)/shard_map/ppermute | solution.py:264
  21.9 9.6 %collective-permute-done.16.refs_10_ = bf16[1536,128]{1,0:T(8,128)(2,1)S(1)} collective-permute-done((bf16[1536,128]{1,0:T(8,128)(2,1)S(1)}, bf16[1536,128]{1,0:T(8,128)(2,1)S(1)}, u32[]{:S(2)}, u32[]{:S(2)}) %collective-permute-start.16) | collective-permute-done | bytes 393248 | tf_op jit(solution)/shard_map/ppermute | solution.py:264
  31.5 4.8 %collective-permute-done.14.refs_8_ = bf16[1536,128]{1,0:T(8,128)(2,1)S(1)} collective-permute-done((bf16[1536,128]{1,0:T(8,128)(2,1)S(1)}, bf16[1536,128]{1,0:T(8,128)(2,1)S(1)}, u32[]{:S(2)}, u32[]{:S(2)}) %collective-permute-start.14) | collective-permute-done | bytes 393248 | tf_op jit(solution)/shard_map/ppermute | solution.py:264
  36.3 2.4 %collective-permute-done.12.refs_6_ = bf16[1536,128]{1,0:T(8,128)(2,1)S(1)} collective-permute-done((bf16[1536,128]{1,0:T(8,128)(2,1)S(1)}, bf16[1536,128]{1,0:T(8,128)(2,1)S(1)}, u32[]{:S(2)}, u32[]{:S(2)}) %collective-permute-start.12) | collective-permute-done | bytes 393248 | tf_op jit(solution)/shard_map/ppermute | solution.py:264
  38.7 1.2 collective-permute-start.9
  39.9 4.7 %collective-permute-done.9.refs_2_ = bf16[512,128]{1,0:T(8,128)(2,1)S(1)} collective-permute-done((bf16[512,128]{1,0:T(8,128)(2,1)S(1)}, bf16[512,128]{1,0:T(8,128)(2,1)S(1)}, u32[]{:S(2)}, u32[]{:S(2)}) %collective-permute-start.9) | collective-permute-done | bytes 131104 | tf_op jit(solution)/shard_map/ppermute | solution.py:264
  45.2 4.5 %collective-permute-done.8.refs_1_ = bf16[512,128]{1,0:T(8,128)(2,1)S(1)} collective-permute-done((bf16[512,128]{1,0:T(8,128)(2,1)S(1)}, bf16[512,128]{1,0:T(8,128)(2,1)S(1)}, u32[]{:S(2)}, u32[]{:S(2)}) %collective-permute-start.8) | collective-permute-done | bytes 131104 | tf_op jit(solution)/shard_map/ppermute | solution.py:264
  49.7 21.5 %attend.1 = (bf16[144,512]{1,0:T(8,128)(2,1)S(1)}, bf16[144,512]{1,0:T(8,128)(2,1)S(1)}, bf16[144,512]{1,0:T(8,128)(2,1)S(1)}, bf16[144,512]{1,0:T(8,128)(2,1)S(1)}) custom-call(s32[1,512]{1,0:T(1,128)S(1)} %bitcast.6, bf16[512,128]{1,0:T(8,128)(2,1)S(1)} %get-tuple-element.12.refs_0_, bf16[512,128]{1,0:T(8,128)(2,1)S(1)} %collective-permute-done.8.refs_1_, ...), custom_call_target="tpu_custom_call" | custom-call | flops 12000000000 | bytes 4000000 | tf_op jit(solution)/shard_map/attend/pallas_call | solution.py:204
  71.3 10.2 %collective-permute-start.19 = (bf16[144,512]{1,0:T(8,128)(2,1)S(1)}, bf16[144,512]{1,0:T(8,128)(2,1)S(1)}, u32[]{:S(2)}, u32[]{:S(2)}) collective-permute-start(bf16[144,512]{1,0:T(8,128)(2,1)S(1)} %get-tuple-element.16), channel_id=1, source_target_pairs={{64,0},{128,64},{192,128},{0,192},{65,1},{129,65},{193,129},{1,193... | collective-permute-start | bytes 442376 | tf_op jit(solution)/shard_map/ppermute | solution.py:264
  81.5 13.8 %collective-permute-start.20 = (bf16[144,512]{1,0:T(8,128)(2,1)S(1)}, bf16[144,512]{1,0:T(8,128)(2,1)S(1)}, u32[]{:S(2)}, u32[]{:S(2)}) collective-permute-start(bf16[144,512]{1,0:T(8,128)(2,1)S(1)} %get-tuple-element.17), channel_id=1, source_target_pairs={{128,0},{192,64},{0,128},{64,192},{129,1},{193,65},{1,129},{65,193... | collective-permute-start | bytes 442376 | tf_op jit(solution)/shard_map/ppermute | solution.py:264
  95.3 1.9 %collective-permute-start = (f32[8,128]{1,0:T(8,128)S(1)}, f32[8,128]{1,0:T(8,128)S(1)}, u32[]{:S(2)}, u32[]{:S(2)}) collective-permute-start(f32[8,128]{1,0:T(8,128)S(1)} %get-tuple-element.11), channel_id=1, source_target_pairs={{0,1},{1,0},{2,3},{3,2},{4,5},{5,4},{6,7},{7,6},{8,9},{9,8},{10,11... | collective-permute-start | bytes 12296 | tf_op jit(solution)/shard_map/ppermute | solution.py:269
  97.3 1.7 %collective-permute-done = f32[8,128]{1,0:T(8,128)S(1)} collective-permute-done((f32[8,128]{1,0:T(8,128)S(1)}, f32[8,128]{1,0:T(8,128)S(1)}, u32[]{:S(2)}, u32[]{:S(2)}) %collective-permute-start) | collective-permute-done | bytes 4128 | tf_op jit(solution)/shard_map/ppermute | solution.py:269
  98.9 3.3 %collective-permute-start.1 = (f32[8,128]{1,0:T(8,128)S(1)}, f32[8,128]{1,0:T(8,128)S(1)}, u32[]{:S(2)}, u32[]{:S(2)}) collective-permute-start(f32[8,128]{1,0:T(8,128)S(1)} %add.40), channel_id=1, source_target_pairs={{0,2},{1,3},{2,0},{3,1},{4,6},{5,7},{6,4},{7,5},{8,10},{9,11},{10,... | collective-permute-start | bytes 12296 | tf_op jit(solution)/shard_map/ppermute | solution.py:269
  102.2 1.6 %collective-permute-done.1 = f32[8,128]{1,0:T(8,128)S(1)} collective-permute-done((f32[8,128]{1,0:T(8,128)S(1)}, f32[8,128]{1,0:T(8,128)S(1)}, u32[]{:S(2)}, u32[]{:S(2)}) %collective-permute-start.1) | collective-permute-done | bytes 4128 | tf_op jit(solution)/shard_map/ppermute | solution.py:269
  103.8 6.8 %collective-permute-start.2 = (f32[8,128]{1,0:T(8,128)S(1)}, f32[8,128]{1,0:T(8,128)S(1)}, u32[]{:S(2)}, u32[]{:S(2)}) collective-permute-start(f32[8,128]{1,0:T(8,128)S(1)} %add.41), channel_id=1, source_target_pairs={{0,4},{1,5},{2,6},{3,7},{4,0},{5,1},{6,2},{7,3},{8,12},{9,13},{10,... | collective-permute-start | bytes 12296 | tf_op jit(solution)/shard_map/ppermute | solution.py:269
  110.7 1.6 %collective-permute-done.2 = f32[8,128]{1,0:T(8,128)S(1)} collective-permute-done((f32[8,128]{1,0:T(8,128)S(1)}, f32[8,128]{1,0:T(8,128)S(1)}, u32[]{:S(2)}, u32[]{:S(2)}) %collective-permute-start.2) | collective-permute-done | bytes 4128 | tf_op jit(solution)/shard_map/ppermute | solution.py:269
  112.3 1.2 collective-permute-done.3
  113.4 3.6 %collective-permute-done.4 = f32[8,128]{1,0:T(8,128)S(1)} collective-permute-done((f32[8,128]{1,0:T(8,128)S(1)}, f32[8,128]{1,0:T(8,128)S(1)}, u32[]{:S(2)}, u32[]{:S(2)}) %collective-permute-start.4) | collective-permute-done | bytes 4128 | tf_op jit(solution)/shard_map/ppermute | solution.py:269
  117.0 5.1 %collective-permute-done.5 = f32[8,128]{1,0:T(8,128)S(1)} collective-permute-done((f32[8,128]{1,0:T(8,128)S(1)}, f32[8,128]{1,0:T(8,128)S(1)}, u32[]{:S(2)}, u32[]{:S(2)}) %collective-permute-start.5) | collective-permute-done | bytes 4128 | tf_op jit(solution)/shard_map/ppermute | solution.py:269
  122.2 3.6 %collective-permute-done.6 = f32[8,128]{1,0:T(8,128)S(1)} collective-permute-done((f32[8,128]{1,0:T(8,128)S(1)}, f32[8,128]{1,0:T(8,128)S(1)}, u32[]{:S(2)}, u32[]{:S(2)}) %collective-permute-start.6) | collective-permute-done | bytes 4128 | tf_op jit(solution)/shard_map/ppermute | solution.py:269
  125.8 5.1 %collective-permute-done.7 = f32[8,128]{1,0:T(8,128)S(1)} collective-permute-done((f32[8,128]{1,0:T(8,128)S(1)}, f32[8,128]{1,0:T(8,128)S(1)}, u32[]{:S(2)}, u32[]{:S(2)}) %collective-permute-start.7) | collective-permute-done | bytes 4128 | tf_op jit(solution)/shard_map/ppermute | solution.py:269
  130.9 1.4 %combine.1 = (bf16[120,512]{1,0:T(8,128)(2,1)}, f32[8,128]{1,0:T(8,128)S(1)}) custom-call(s32[4]{0:T(128)S(1)} %copy-done.7, f32[8,128]{1,0:T(8,128)S(1)} %pad_maximum_fusion.dev, bf16[144,512]{1,0:T(8,128)(2,1)S(1)} %get-tuple-element.14.p0, bf16[144,512]{1,0:T(8,128)(2,1)S(1)} %collective-permute-done.18.p1, ...), custom_call_target="tpu_custom_call" | custom-call | flops 1000000 | bytes 1000000 | tf_op jit(solution)/shard_map/combine/pallas_call | solution.py:248
  (43 shorter events, 1.9 us)
Async XLA Ops:
  1.4 2.8 %copy-start = (bf16[768,4096]{1,0:T(8,128)(2,1)S(1)}, bf16[768,4096]{1,0:T(8,128)(2,1)}, u32[]{:S(2)}) copy-start(bf16[768,4096]{1,0:T(8,128)(2,1)} %hidden.1) | copy-start | bytes 18874372
  4.2 2.2 %copy-start.1 = (bf16[4096,512]{1,0:T(8,128)(2,1)S(1)}, bf16[4096,512]{1,0:T(8,128)(2,1)}, u32[]{:S(2)}) copy-start(bf16[4096,512]{1,0:T(8,128)(2,1)} %w_query.1) | copy-start | bytes 12582916
  6.4 1.2 copy-start.2
  7.6 1.2 copy-start.3
  8.8 0.9 copy-start.4
  9.8 0.9 copy-start.5
  10.7 0.7 copy-start.6
  17.9 13.6 %collective-permute-start.16 = (bf16[1536,128]{1,0:T(8,128)(2,1)S(1)}, bf16[1536,128]{1,0:T(8,128)(2,1)S(1)}, u32[]{:S(2)}, u32[]{:S(2)}) collective-permute-start(bf16[1536,128]{1,0:T(8,128)(2,1)S(1)} %get-tuple-element.13.refs_4_), channel_id=1, source_target_pairs={{32,0},{48,16},{0,32},{16,48},{33,1},{49,17},{1,33},{17,49},{34,2}... | collective-permute-start | bytes 1179656 | tf_op jit(solution)/shard_map/ppermute | solution.py:264
  19.2 17.2 %collective-permute-start.14 = (bf16[1536,128]{1,0:T(8,128)(2,1)S(1)}, bf16[1536,128]{1,0:T(8,128)(2,1)S(1)}, u32[]{:S(2)}, u32[]{:S(2)}) collective-permute-start(bf16[1536,128]{1,0:T(8,128)(2,1)S(1)} %get-tuple-element.13.refs_4_), channel_id=1, source_target_pairs={{48,0},{0,16},{16,32},{32,48},{49,1},{1,17},{17,33},{33,49},{50,2}... | collective-permute-start | bytes 1179656 | tf_op jit(solution)/shard_map/ppermute | solution.py:264
  21.3 17.4 %collective-permute-start.12 = (bf16[1536,128]{1,0:T(8,128)(2,1)S(1)}, bf16[1536,128]{1,0:T(8,128)(2,1)S(1)}, u32[]{:S(2)}, u32[]{:S(2)}) collective-permute-start(bf16[1536,128]{1,0:T(8,128)(2,1)S(1)} %get-tuple-element.13.refs_4_), channel_id=1, source_target_pairs={{16,0},{32,16},{48,32},{0,48},{17,1},{33,17},{49,33},{1,49},{18,2}... | collective-permute-start | bytes 1179656 | tf_op jit(solution)/shard_map/ppermute | solution.py:264
  21.3 17.4 %collective-permute-start.10 = (bf16[512,128]{1,0:T(8,128)(2,1)S(1)}, bf16[512,128]{1,0:T(8,128)(2,1)S(1)}, u32[]{:S(2)}, u32[]{:S(2)}) collective-permute-start(bf16[512,128]{1,0:T(8,128)(2,1)S(1)} %get-tuple-element.12.refs_0_), channel_id=1, source_target_pairs={{128,0},{192,64},{0,128},{64,192},{129,1},{193,65},{1,129},{65,193... | collective-permute-start | bytes 393224 | tf_op jit(solution)/shard_map/ppermute | solution.py:264
  21.9 27.8 %collective-permute-start.11 = (bf16[1536,128]{1,0:T(8,128)(2,1)S(1)}, bf16[1536,128]{1,0:T(8,128)(2,1)S(1)}, u32[]{:S(2)}, u32[]{:S(2)}) collective-permute-start(bf16[1536,128]{1,0:T(8,128)(2,1)S(1)} %get-tuple-element.13.refs_4_), channel_id=1, source_target_pairs={{0,8},{8,0},{1,9},{9,1},{2,10},{10,2},{3,11},{11,3},{4,12},{12,4},... | collective-permute-start | bytes 1179656 | tf_op jit(solution)/shard_map/ppermute | solution.py:269
  31.5 18.2 %collective-permute-start.17 = (bf16[1536,128]{1,0:T(8,128)(2,1)S(1)}, bf16[1536,128]{1,0:T(8,128)(2,1)S(1)}, u32[]{:S(2)}, u32[]{:S(2)}) collective-permute-start(bf16[1536,128]{1,0:T(8,128)(2,1)S(1)} %collective-permute-done.16.refs_10_), channel_id=1, source_target_pairs={{0,8},{8,0},{1,9},{9,1},{2,10},{10,2},{3,11},{11,3},{4,12},{12,4},... | collective-permute-start | bytes 1179656 | tf_op jit(solution)/shard_map/ppermute | solution.py:269
  36.3 13.4 %collective-permute-start.15 = (bf16[1536,128]{1,0:T(8,128)(2,1)S(1)}, bf16[1536,128]{1,0:T(8,128)(2,1)S(1)}, u32[]{:S(2)}, u32[]{:S(2)}) collective-permute-start(bf16[1536,128]{1,0:T(8,128)(2,1)S(1)} %collective-permute-done.14.refs_8_), channel_id=1, source_target_pairs={{0,8},{8,0},{1,9},{9,1},{2,10},{10,2},{3,11},{11,3},{4,12},{12,4},... | collective-permute-start | bytes 1179656 | tf_op jit(solution)/shard_map/ppermute | solution.py:269
  38.7 11.0 %collective-permute-start.13 = (bf16[1536,128]{1,0:T(8,128)(2,1)S(1)}, bf16[1536,128]{1,0:T(8,128)(2,1)S(1)}, u32[]{:S(2)}, u32[]{:S(2)}) collective-permute-start(bf16[1536,128]{1,0:T(8,128)(2,1)S(1)} %collective-permute-done.12.refs_6_), channel_id=1, source_target_pairs={{0,8},{8,0},{1,9},{9,1},{2,10},{10,2},{3,11},{11,3},{4,12},{12,4},... | collective-permute-start | bytes 1179656 | tf_op jit(solution)/shard_map/ppermute | solution.py:269
  38.7 5.9 %collective-permute-start.9 = (bf16[512,128]{1,0:T(8,128)(2,1)S(1)}, bf16[512,128]{1,0:T(8,128)(2,1)S(1)}, u32[]{:S(2)}, u32[]{:S(2)}) collective-permute-start(bf16[512,128]{1,0:T(8,128)(2,1)S(1)} %get-tuple-element.12.refs_0_), channel_id=1, source_target_pairs={{192,0},{0,64},{64,128},{128,192},{193,1},{1,65},{65,129},{129,193... | collective-permute-start | bytes 393224 | tf_op jit(solution)/shard_map/ppermute | solution.py:264
  44.6 5.0 %collective-permute-start.8 = (bf16[512,128]{1,0:T(8,128)(2,1)S(1)}, bf16[512,128]{1,0:T(8,128)(2,1)S(1)}, u32[]{:S(2)}, u32[]{:S(2)}) collective-permute-start(bf16[512,128]{1,0:T(8,128)(2,1)S(1)} %get-tuple-element.12.refs_0_), channel_id=1, source_target_pairs={{64,0},{128,64},{192,128},{0,192},{65,1},{129,65},{193,129},{1,193... | collective-permute-start | bytes 393224 | tf_op jit(solution)/shard_map/ppermute | solution.py:264
  49.7 81.2 %copy-start.7 = (s32[4]{0:T(128)S(1)}, s32[4]{0:T(128)}, u32[]{:S(2)}) copy-start(s32[4]{0:T(128)} %lengths.3) | copy-start | bytes 52
  71.3 59.6 %collective-permute-start.18 = (bf16[144,512]{1,0:T(8,128)(2,1)S(1)}, bf16[144,512]{1,0:T(8,128)(2,1)S(1)}, u32[]{:S(2)}, u32[]{:S(2)}) collective-permute-start(bf16[144,512]{1,0:T(8,128)(2,1)S(1)} %get-tuple-element.15), channel_id=1, source_target_pairs={{192,0},{0,64},{64,128},{128,192},{193,1},{1,65},{65,129},{129,193... | collective-permute-start | bytes 442376 | tf_op jit(solution)/shard_map/ppermute | solution.py:264
  71.3 59.6 %collective-permute-start.19 = (bf16[144,512]{1,0:T(8,128)(2,1)S(1)}, bf16[144,512]{1,0:T(8,128)(2,1)S(1)}, u32[]{:S(2)}, u32[]{:S(2)}) collective-permute-start(bf16[144,512]{1,0:T(8,128)(2,1)S(1)} %get-tuple-element.16), channel_id=1, source_target_pairs={{64,0},{128,64},{192,128},{0,192},{65,1},{129,65},{193,129},{1,193... | collective-permute-start | bytes 442376 | tf_op jit(solution)/shard_map/ppermute | solution.py:264
  81.5 49.4 %collective-permute-start.20 = (bf16[144,512]{1,0:T(8,128)(2,1)S(1)}, bf16[144,512]{1,0:T(8,128)(2,1)S(1)}, u32[]{:S(2)}, u32[]{:S(2)}) collective-permute-start(bf16[144,512]{1,0:T(8,128)(2,1)S(1)} %get-tuple-element.17), channel_id=1, source_target_pairs={{128,0},{192,64},{0,128},{64,192},{129,1},{193,65},{1,129},{65,193... | collective-permute-start | bytes 442376 | tf_op jit(solution)/shard_map/ppermute | solution.py:264
  95.3 3.6 %collective-permute-start = (f32[8,128]{1,0:T(8,128)S(1)}, f32[8,128]{1,0:T(8,128)S(1)}, u32[]{:S(2)}, u32[]{:S(2)}) collective-permute-start(f32[8,128]{1,0:T(8,128)S(1)} %get-tuple-element.11), channel_id=1, source_target_pairs={{0,1},{1,0},{2,3},{3,2},{4,5},{5,4},{6,7},{7,6},{8,9},{9,8},{10,11... | collective-permute-start | bytes 12296 | tf_op jit(solution)/shard_map/ppermute | solution.py:269
  98.9 4.9 %collective-permute-start.1 = (f32[8,128]{1,0:T(8,128)S(1)}, f32[8,128]{1,0:T(8,128)S(1)}, u32[]{:S(2)}, u32[]{:S(2)}) collective-permute-start(f32[8,128]{1,0:T(8,128)S(1)} %add.40), channel_id=1, source_target_pairs={{0,2},{1,3},{2,0},{3,1},{4,6},{5,7},{6,4},{7,5},{8,10},{9,11},{10,... | collective-permute-start | bytes 12296 | tf_op jit(solution)/shard_map/ppermute | solution.py:269
  103.8 8.4 %collective-permute-start.2 = (f32[8,128]{1,0:T(8,128)S(1)}, f32[8,128]{1,0:T(8,128)S(1)}, u32[]{:S(2)}, u32[]{:S(2)}) collective-permute-start(f32[8,128]{1,0:T(8,128)S(1)} %add.41), channel_id=1, source_target_pairs={{0,4},{1,5},{2,6},{3,7},{4,0},{5,1},{6,2},{7,3},{8,12},{9,13},{10,... | collective-permute-start | bytes 12296 | tf_op jit(solution)/shard_map/ppermute | solution.py:269
  112.3 1.2 collective-permute-start.3
  113.4 3.6 %collective-permute-start.4 = (f32[8,128]{1,0:T(8,128)S(1)}, f32[8,128]{1,0:T(8,128)S(1)}, u32[]{:S(2)}, u32[]{:S(2)}) collective-permute-start(f32[8,128]{1,0:T(8,128)S(1)} %add.43), channel_id=1, source_target_pairs={{0,16},{16,0},{32,48},{48,32},{1,17},{17,1},{33,49},{49,33},{2,18}... | collective-permute-start | bytes 12296 | tf_op jit(solution)/shard_map/ppermute | solution.py:269
  117.0 5.1 %collective-permute-start.5 = (f32[8,128]{1,0:T(8,128)S(1)}, f32[8,128]{1,0:T(8,128)S(1)}, u32[]{:S(2)}, u32[]{:S(2)}) collective-permute-start(f32[8,128]{1,0:T(8,128)S(1)} %add.44), channel_id=1, source_target_pairs={{0,32},{16,48},{32,0},{48,16},{1,33},{17,49},{33,1},{49,17},{2,34}... | collective-permute-start | bytes 12296 | tf_op jit(solution)/shard_map/ppermute | solution.py:269
  122.2 3.6 %collective-permute-start.6 = (f32[8,128]{1,0:T(8,128)S(1)}, f32[8,128]{1,0:T(8,128)S(1)}, u32[]{:S(2)}, u32[]{:S(2)}) collective-permute-start(f32[8,128]{1,0:T(8,128)S(1)} %add.45), channel_id=1, source_target_pairs={{0,64},{64,0},{128,192},{192,128},{1,65},{65,1},{129,193},{193,129... | collective-permute-start | bytes 12296 | tf_op jit(solution)/shard_map/ppermute | solution.py:269
  125.8 5.1 %collective-permute-start.7 = (f32[8,128]{1,0:T(8,128)S(1)}, f32[8,128]{1,0:T(8,128)S(1)}, u32[]{:S(2)}, u32[]{:S(2)}) collective-permute-start(f32[8,128]{1,0:T(8,128)S(1)} %add.46), channel_id=1, source_target_pairs={{0,128},{64,192},{128,0},{192,64},{1,129},{65,193},{129,1},{193,65... | collective-permute-start | bytes 12296 | tf_op jit(solution)/shard_map/ppermute | solution.py:269

commit v2 on v0

v2 whole, which is shorter than its diff:
```python
import functools
import math

import jax
import jax.numpy as jnp
from jax import lax
from jax.experimental import pallas as pl
from jax.experimental.pallas import tpu as pltpu
from jax.sharding import Mesh, PartitionSpec as P


HEAD_DIM = 128
GROUP = 4
TOK = 768
SEL = 120
ROWS = 128
QROWS = GROUP * ROWS
DOCS = 4
CHUNK = 1024
NEG = -1e30
EXP_SCALE = (HEAD_DIM ** -0.5) * math.log2(math.e)
SEQ = ("x", "y", "c")
f32, bf16 = jnp.float32, jnp.bfloat16


def seq_number():
    return (lax.axis_index("x") * 4 + lax.axis_index("y")) * 2 + lax.axis_index("c")


def doc_ends(lengths):
    ends = [lengths[0]]
    for d in range(1, DOCS):
        ends.append(ends[-1] + lengths[d])
    return ends


def project_kernel(lengths, selected, hidden, w_query, w_key, w_value, cached_key, cached_value,
                   kv_out, q_out, dev_out, mask_out,
                   states, wq, wkv, old, chosen_rows, acc_kv, acc_q, sem, one_sem):
    steps = hidden.shape[1] // CHUNK
    fetch_rows = pltpu.make_async_copy(selected, chosen_rows, one_sem.at[0])
    fetch_rows.start()
    copies = []
    for k in range(steps):
        part = pl.ds(k * CHUNK, CHUNK)
        copies.append([
            pltpu.make_async_copy(hidden.at[:, part], states.at[k], sem.at[0, k]),
            pltpu.make_async_copy(w_key.at[part, :], wkv.at[k, :, pl.ds(0, HEAD_DIM)], sem.at[1, k]),
            pltpu.make_async_copy(w_value.at[part, :], wkv.at[k, :, pl.ds(HEAD_DIM, HEAD_DIM)], sem.at[2, k]),
            pltpu.make_async_copy(w_query.at[part, :], wq.at[k], sem.at[3, k]),
        ])
        for copy in copies[-1]:
            copy.start()
    olds = [
        pltpu.make_async_copy(cached_key, old.at[0], one_sem.at[1]),
        pltpu.make_async_copy(cached_value, old.at[1], one_sem.at[2]),
    ]
    for copy in olds:
        copy.start()
    fetch_rows.wait()
    base = seq_number() * SEL
    lane = lax.broadcasted_iota(jnp.int32, (1, ROWS), 1)
    pieces = [jnp.full((1, ROWS), -1, jnp.int32) for _ in range(4)]
    for r in range(SEL):
        pieces[r % 4] = jnp.where(lane == r, chosen_rows[base + r], pieces[r % 4])
    own = functools.reduce(jnp.maximum, pieces)
    mask_out[...] = jnp.concatenate([jnp.where(lane < SEL, own, TOK)] * GROUP, axis=1)
    across = jnp.broadcast_to(own, (ROWS, ROWS)).astype(f32).T
    tokens = lax.broadcasted_iota(jnp.int32, (ROWS, TOK), 1).astype(f32)
    pick = jnp.where(jnp.concatenate([across] * (TOK // ROWS), axis=1) == tokens, 1.0, 0.0).astype(bf16)
    acc_kv[...] = jnp.zeros_like(acc_kv)
    acc_q[...] = jnp.zeros_like(acc_q)
    for k in range(steps):
        for copy in copies[k]:
            copy.wait()
        acc_kv[...] += jnp.dot(states[k], wkv[k], preferred_element_type=f32)
        picked = jnp.dot(pick, states[k], preferred_element_type=f32).astype(bf16)
        acc_q[...] += jnp.dot(picked, wq[k], preferred_element_type=f32)
    for copy in olds:
        copy.wait()
    for h in range(GROUP):
        q_out[h * ROWS:(h + 1) * ROWS, :] = (
            acc_q[:, h * HEAD_DIM:(h + 1) * HEAD_DIM] * EXP_SCALE).astype(bf16)
    first = seq_number() * TOK
    ends = doc_ends(lengths)
    totals = [jnp.zeros((1, ROWS), f32) for _ in range(DOCS)]
    for t in range(TOK // ROWS):
        part = slice(t * ROWS, (t + 1) * ROWS)
        place = lax.broadcasted_iota(jnp.int32, (ROWS, ROWS), 0) + t * ROWS
        chosen = jnp.max(jnp.where(place == own, 1.0, 0.0), axis=1, keepdims=True) > 0.0
        old_key = old[0, part, :].astype(f32)
        old_value = old[1, part, :].astype(f32)
        new_key = acc_kv[part, :HEAD_DIM]
        new_value = acc_kv[part, HEAD_DIM:]
        kv_out[part, :] = jnp.where(chosen, new_key, old_key).astype(bf16)
        kv_out[TOK + t * ROWS:TOK + (t + 1) * ROWS, :] = jnp.where(chosen, new_value, old_value).T.astype(bf16)
        shift = (new_key - old_key) ** 2 + (new_value - old_value) ** 2
        dev = jnp.sum(shift.T, axis=0, keepdims=True)
        dev_out[t:t + 1, :] = dev
        at = lane + (first + t * ROWS)
        doc = sum([(at >= e).astype(jnp.int32) for e in ends])
        for d in range(DOCS):
            totals[d] = totals[d] + jnp.where(doc == d, dev, 0.0)
    row = jnp.zeros((1, ROWS), f32)
    for d in range(DOCS):
        row = jnp.where(lane == d, jnp.sum(totals[d], axis=1, keepdims=True), row)
    dev_out[6:7, :] = row
    dev_out[7:8, :] = jnp.zeros((1, ROWS), f32)


def project(lengths, selected, hidden, w_query, w_key, w_value, cached_key, cached_value):
    steps = hidden.shape[1] // CHUNK
    hbm = pl.BlockSpec(memory_space=pltpu.HBM)
    vmem = pl.BlockSpec(memory_space=pltpu.VMEM)
    return pl.pallas_call(
        project_kernel,
        in_specs=[pl.BlockSpec(memory_space=pltpu.SMEM)] + [hbm] * 7,
        out_specs=[vmem] * 4,
        out_shape=[
            jax.ShapeDtypeStruct((2 * TOK, HEAD_DIM), bf16),
            jax.ShapeDtypeStruct((QROWS, HEAD_DIM), bf16),
            jax.ShapeDtypeStruct((8, ROWS), f32),
            jax.ShapeDtypeStruct((1, QROWS), jnp.int32),
        ],
        scratch_shapes=[
            pltpu.VMEM((steps, TOK, CHUNK), bf16),
            pltpu.VMEM((steps, CHUNK, GROUP * HEAD_DIM), bf16),
            pltpu.VMEM((steps, CHUNK, 2 * HEAD_DIM), bf16),
            pltpu.VMEM((2, TOK, HEAD_DIM), bf16),
            pltpu.SMEM(selected.shape, jnp.int32),
            pltpu.VMEM((TOK, 2 * HEAD_DIM), f32),
            pltpu.VMEM((ROWS, GROUP * HEAD_DIM), f32),
            pltpu.SemaphoreType.DMA((4, steps)),
            pltpu.SemaphoreType.DMA((3,)),
        ],
        compiler_params=pltpu.CompilerParams(vmem_limit_bytes=66_400_000),
        cost_estimate=pl.CostEstimate(flops=5 * 10**9, bytes_accessed=13 * 10**6, transcendentals=0),
        name="project",
    )(lengths, selected, hidden, w_query, w_key, w_value, cached_key, cached_value)


X_STEPS = (0, 1, 3, 2)
Y_STEPS = (0, 1, 3, 2)
ACC = HEAD_DIM + 16


def score_tile(q, kv, i, j, s_ref, top_ref):
    s = lax.dot_general(kv[j, :TOK, :], q[i], (((1,), (1,)), ((), ())), preferred_element_type=f32)
    s_ref[...] = s
    top_ref[...] = jnp.max(s.reshape(TOK // 8, 8, QROWS), axis=0)


def mix_tile(kv, m_s, acc_s, i, j, s_ref, top_ref):
    old = m_s[i, 0:1, :]
    new = jnp.maximum(old, jnp.max(top_ref[...], axis=0, keepdims=True))
    m_s[i, 0:1, :] = new
    p = jnp.exp2(s_ref[...] - new).astype(bf16)
    values = jnp.concatenate(
        [kv[j, TOK + k * ROWS:TOK + (k + 1) * ROWS, :] for k in range(TOK // ROWS)], axis=1)
    values = jnp.concatenate([values, jnp.ones((16, TOK), bf16)], axis=0)
    acc_s[i] = acc_s[i] * jnp.exp2(old - new) + jnp.dot(values, p, preferred_element_type=f32)


def attend_kernel(dy, first, last, *refs):
    n = 2
    refs = list(refs)
    mask_rows = refs.pop(0) if first else None
    q_in, refs = refs[:4], refs[4:]
    kv_in, refs = refs[:n], refs[n:]
    if not first:
        m_in, acc_in, refs = refs[0], refs[1], refs[2:]
    if last:
        outs, refs = refs[:4], refs[4:]
        m_s, acc_s, refs = refs[0], refs[1], refs[2:]
    else:
        m_s, acc_s, refs = refs[0], refs[1], refs[2:]
    q, kv, s_a, s_b, top_a, top_b, pairs = refs
    for i in range(4):
        q[i] = q_in[i][...]
    for j in range(n):
        kv[j] = kv_in[j][...]
    if first:
        m_s[...] = jnp.full_like(m_s, NEG)
        acc_s[...] = jnp.zeros_like(acc_s)
        place = lax.broadcasted_iota(jnp.int32, (TOK, QROWS), 0)
        s = lax.dot_general(kv[0, :TOK, :], q[0], (((1,), (1,)), ((), ())), preferred_element_type=f32)
        s = jnp.where(place <= mask_rows[...], s, NEG)
        s_a[...] = s
        top_a[...] = jnp.max(s.reshape(TOK // 8, 8, QROWS), axis=0)
        mix_tile(kv, m_s, acc_s, 0, 0, s_a, top_a)
    else:
        m_s[...] = m_in[...]
        acc_s[...] = acc_in[...]
    x, y, c = lax.axis_index("x"), lax.axis_index("y"), lax.axis_index("c")
    count = jnp.int32(0)
    for i, dx in enumerate(X_STEPS):
        for j, dc in enumerate((0, 1)):
            q_at = ((x + dx) & 3) * 8 + 2 * y + c
            kv_at = x * 8 + 2 * ((y + dy) & 3) + ((c + dc) & 1)
            pairs[count] = i * 8 + j
            count = count + jnp.where(q_at > kv_at, 1, 0)

    def pair(k):
        v = pairs[jnp.minimum(k, count - 1)]
        return v >> 3, v & 7

    @pl.when(count > 0)
    def _():
        score_tile(q, kv, *pair(0), s_a, top_a)

    @pl.loop(0, (count + 1) >> 1)
    def _(h):
        k = h * 2
        score_tile(q, kv, *pair(k + 1), s_b, top_b)
        mix_tile(kv, m_s, acc_s, *pair(k), s_a, top_a)

        @pl.when(k + 1 < count)
        def _():
            score_tile(q, kv, *pair(k + 2), s_a, top_a)
            mix_tile(kv, m_s, acc_s, *pair(k + 1), s_b, top_b)

    if last:
        for i in range(4):
            total = acc_s[i, HEAD_DIM:HEAD_DIM + 1, :]
            safe = jnp.maximum(total, 1e-30)
            outs[i][:HEAD_DIM, :] = (acc_s[i, :HEAD_DIM, :] * (1.0 / safe)).astype(bf16)
            lse = jnp.where(total > 0.0, m_s[i, 0:1, :] + jnp.log2(safe), NEG)
            outs[i][HEAD_DIM:, :] = jnp.concatenate(
                split3(lse) + [jnp.zeros((13, QROWS), f32)], axis=0).astype(bf16)


def split3(value):
    high = value.astype(bf16).astype(f32)
    mid = (value - high).astype(bf16).astype(f32)
    return [high, mid, value - high - mid]


def attend(dy, last, qs, kvs, mask_rows, state):
    first = state is None
    n = 2
    vmem = pl.BlockSpec(memory_space=pltpu.VMEM)
    args = ([mask_rows] if first else []) + list(qs) + list(kvs)
    args += [] if first else list(state)
    states = [jax.ShapeDtypeStruct((4, 8, QROWS), f32), jax.ShapeDtypeStruct((4, ACC, QROWS), f32)]
    keep = [pltpu.VMEM((4, 8, QROWS), f32), pltpu.VMEM((4, ACC, QROWS), f32)]
    return pl.pallas_call(
        functools.partial(attend_kernel, dy, first, last),
        in_specs=[vmem] * len(args),
        out_specs=[vmem] * (4 if last else 2),
        out_shape=[jax.ShapeDtypeStruct((ACC, QROWS), bf16)] * 4 if last else states,
        scratch_shapes=(keep if last else []) + [
            pltpu.VMEM((4, QROWS, HEAD_DIM), bf16),
            pltpu.VMEM((n, 2 * TOK, HEAD_DIM), bf16),
            pltpu.VMEM((TOK, QROWS), f32),
            pltpu.VMEM((TOK, QROWS), f32),
            pltpu.VMEM((8, QROWS), f32),
            pltpu.VMEM((8, QROWS), f32),
            pltpu.SMEM((40,), jnp.int32),
        ],
        compiler_params=pltpu.CompilerParams(vmem_limit_bytes=30 * 2**20),
        cost_estimate=pl.CostEstimate(flops=n * 4 * 10**9, bytes_accessed=4 * 10**6, transcendentals=10**6),
        name="attend",
    )(*args)


def combine_kernel(lengths, dev, docs, p0, p1, p2, p3, out, score):
    parts = (p0, p1, p2, p3)
    rows = [p[HEAD_DIM:HEAD_DIM + 16, :].astype(f32) for p in parts]
    lses = [v[0:1] + v[1:2] + v[2:3] for v in rows]
    total = docs[6:7, :]
    top = functools.reduce(jnp.maximum, lses)
    weights = [jnp.exp2(v - top) for v in lses]
    scale = 1.0 / sum(weights)
    mixed = sum([p[:HEAD_DIM, :].astype(f32) * (w * scale) for p, w in zip(parts, weights)])
    for h in range(GROUP):
        out[:, h * HEAD_DIM:(h + 1) * HEAD_DIM] = (
            mixed[:, h * ROWS:(h + 1) * ROWS].T[:SEL, :].astype(bf16))
    first = seq_number() * TOK
    ends = doc_ends(lengths)
    lane = lax.broadcasted_iota(jnp.int32, (8, ROWS), 1)
    place = lane + lax.broadcasted_iota(jnp.int32, (8, ROWS), 0) * ROWS + first
    doc = sum([(place >= e).astype(jnp.int32) for e in ends])
    mean = jnp.zeros((8, ROWS), f32)
    for d in range(DOCS):
        mean = jnp.where(doc == d, total[:, d:d + 1] / lengths[d].astype(f32), mean)
    score[...] = dev[...] / (mean + 1.0)


def combine(lengths, dev, docs, parts):
    vmem = pl.BlockSpec(memory_space=pltpu.VMEM)
    return pl.pallas_call(
        combine_kernel,
        in_specs=[pl.BlockSpec(memory_space=pltpu.SMEM)] + [vmem] * 6,
        out_specs=[vmem, vmem],
        out_shape=[
            jax.ShapeDtypeStruct((SEL, GROUP * HEAD_DIM), bf16),
            jax.ShapeDtypeStruct((8, ROWS), f32),
        ],
        compiler_params=pltpu.CompilerParams(vmem_limit_bytes=8 * 2**20),
        cost_estimate=pl.CostEstimate(flops=10**6, bytes_accessed=10**6, transcendentals=0),
        name="combine",
    )(lengths, dev, docs, *parts)


def fetch(value, axis, step):
    size = lax.axis_size(axis)
    return lax.ppermute(value, axis, [((i + step) % size, i) for i in range(size)])


def exchange(value, axis, bit):
    size = lax.axis_size(axis)
    return lax.ppermute(value, axis, [(i, i ^ bit) for i in range(size)])


def program(hidden, w_query, w_key, w_value, cached_key, cached_value, doc_lengths, selected):
    kv, q, dev, mask_rows = project(
        doc_lengths, selected, hidden, w_query, w_key, w_value, cached_key, cached_value)
    kv_y, kv_c, qs = {0: kv}, {}, [q]
    for s in (1, 3, 2):
        kv_y[s] = fetch(kv, "y", s)
    for s in X_STEPS[1:]:
        qs.append(fetch(q, "x", s))
    for s in (0, 1, 3, 2):
        kv_c[s] = exchange(kv_y[s], "c", 1)
    for bit in (1, 2, 4):
        dev = dev + exchange(dev, "kvh", bit)
    docs = dev
    for axis, bit in (("c", 1), ("y", 1), ("y", 2), ("x", 1), ("x", 2)):
        docs = docs + exchange(docs, axis, bit)
    state = None
    for n, s in enumerate(Y_STEPS):
        state = attend(s, n == len(Y_STEPS) - 1, qs, [kv_y[s], kv_c[s]], mask_rows, state)
    mine = [state[0]]
    for n, s in enumerate(X_STEPS[1:]):
        mine.append(fetch(state[n + 1], "x", (4 - s) % 4))
    attended, score = combine(doc_lengths, dev, docs, mine)
    return attended, score.reshape(-1)[:TOK]


def solution(mesh):
    fine = Mesh(mesh.devices.reshape(4, 4, 2, 8), ("x", "y", "c", "kvh"))
    return jax.shard_map(
        program,
        mesh=fine,
        in_specs=(
            P(SEQ, None),
            P(None, "kvh"),
            P(None, "kvh"),
            P(None, "kvh"),
            P(SEQ, "kvh"),
            P(SEQ, "kvh"),
            P(),
            P(),
        ),
        out_specs=(P(SEQ, "kvh"), P(SEQ)),
        check_vma=False,
    )
```

time: 164 us -> 93.8 us (0.57)
  the two profiles are of different devices: /device:TPU:1 before, /device:TPU:12 now
where the time goes in v2:
time: 93.8 us; the launch traced here: 93.6 us
  starting transfers between devices  37.5 us (40%)
  waiting for transfers between devices  34.6 us (37%)
  Pallas kernels  17.6 us (19%)
  local copies, waits for them, and re-layouts  3.19 us (3%)
    ppermute x9, starting transfers between devices, fetch(): lax.ppermute(value, axis, [((i + step) % size, i) for i in range(size)])  22.9 us
    ppermute x12, waiting for transfers between devices, exchange(): return lax.ppermute(value, axis, [(i, i ^ bit) for i in range(size)])  21.4 us
    ppermute x12, starting transfers between devices, exchange(): return lax.ppermute(value, axis, [(i, i ^ bit) for i in range(size)])  14.6 us
    ppermute x9, waiting for transfers between devices, fetch(): lax.ppermute(value, axis, [((i + step) % size, i) for i in range(size)])  13.1 us
    pallas_call x4, Pallas kernels, attend(): pl.pallas_call(functools.partial(attend_kernel, dy, first, last), in_spec...  8.28 us
    pallas_call x1, Pallas kernels, project(): pl.pallas_call(project_kernel, in_specs=[pl.BlockSpec(memory_space=pltpu....  7.95 us
    unnamed x12, local copies, waits for them, and re-layouts  2.6 us
  transfers between devices with their start and end apart: 21, of which 12 were waited for; matrix products, arithmetic and copies ran while one was open for 0% of the time, Pallas kernels for 7%

profile of v2, /device:TPU:12, one launch (start us, length us, event | category | flops | bytes accessed | tf_op | source)
XLA Modules:
  0.0 93.6 jit_solution(4194096618358330404)
XLA Ops:
  0.6 8.0 %project.1 = (bf16[1536,128]{1,0:T(8,128)(2,1)}, bf16[512,128]{1,0:T(8,128)(2,1)}, f32[8,128]{1,0:T(8,128)}, s32[1,512]{1,0:T(1,128)}) custom-call(s32[4]{0:T(128)} %lengths.3, s32[3840]{0:T(1024)} %selected.1, bf16[768,4096]{1,0:T(8,128)(2,1)} %hidden.1, bf16[4096,512]{1,0:T(8,128)(2,1)} %w_query.1, bf16[4096,128]{1,0:T(8,128)(2,1)} %w_key.1, ...), custom_call_target="tpu_custom_call" | custom-call | flops 5000000000 | bytes 13000000 | tf_op jit(solution)/shard_map/project/pallas_call | solution.py:115
  8.6 0.5 collective-permute-start.15
  9.1 1.6 %collective-permute-start.13 = (bf16[1536,128]{1,0:T(8,128)(2,1)}, bf16[1536,128]{1,0:T(8,128)(2,1)S(1)}, u32[]{:S(2)}, u32[]{:S(2)}) collective-permute-start(bf16[1536,128]{1,0:T(8,128)(2,1)} %get-tuple-element.20.refs_5_), channel_id=1, source_target_pairs={{48,0},{0,16},{16,32},{32,48},{49,1},{1,17},{17,33},{33,49},{50,2}... | collective-permute-start | bytes 1179656 | tf_op jit(solution)/shard_map/ppermute | solution.py:307
  10.7 3.5 %collective-permute-start.11 = (bf16[1536,128]{1,0:T(8,128)(2,1)}, bf16[1536,128]{1,0:T(8,128)(2,1)S(1)}, u32[]{:S(2)}, u32[]{:S(2)}) collective-permute-start(bf16[1536,128]{1,0:T(8,128)(2,1)} %get-tuple-element.20.refs_5_), channel_id=1, source_target_pairs={{32,0},{48,16},{0,32},{16,48},{33,1},{49,17},{1,33},{17,49},{34,2}... | collective-permute-start | bytes 1179656 | tf_op jit(solution)/shard_map/ppermute | solution.py:307
  14.7 6.2 %collective-permute-done.10.refs_4_.refs_3_ = bf16[512,128]{1,0:T(8,128)(2,1)S(1)} collective-permute-done((bf16[512,128]{1,0:T(8,128)(2,1)}, bf16[512,128]{1,0:T(8,128)(2,1)S(1)}, u32[]{:S(2)}, u32[]{:S(2)}) %collective-permute-start.10) | collective-permute-done | bytes 131104 | tf_op jit(solution)/shard_map/ppermute | solution.py:307
  20.9 0.5 collective-permute-start.8
  21.4 4.6 %collective-permute-done.8.refs_2_.refs_1_ = bf16[512,128]{1,0:T(8,128)(2,1)S(1)} collective-permute-done((bf16[512,128]{1,0:T(8,128)(2,1)}, bf16[512,128]{1,0:T(8,128)(2,1)S(1)}, u32[]{:S(2)}, u32[]{:S(2)}) %collective-permute-start.8) | collective-permute-done | bytes 131104 | tf_op jit(solution)/shard_map/ppermute | solution.py:307
  26.1 2.4 %collective-permute-start.9 = (bf16[512,128]{1,0:T(8,128)(2,1)}, bf16[512,128]{1,0:T(8,128)(2,1)S(1)}, u32[]{:S(2)}, u32[]{:S(2)}) collective-permute-start(bf16[512,128]{1,0:T(8,128)(2,1)} %get-tuple-element.19.refs_1_.refs_0_), channel_id=1, source_target_pairs={{192,0},{0,64},{64,128},{128,192},{193,1},{1,65},{65,129},{129,193... | collective-permute-start | bytes 393224 | tf_op jit(solution)/shard_map/ppermute | solution.py:307
  29.2 2.1 %collective-permute-done.9.refs_3_.refs_2_ = bf16[512,128]{1,0:T(8,128)(2,1)S(1)} collective-permute-done((bf16[512,128]{1,0:T(8,128)(2,1)}, bf16[512,128]{1,0:T(8,128)(2,1)S(1)}, u32[]{:S(2)}, u32[]{:S(2)}) %collective-permute-start.9) | collective-permute-done | bytes 131104 | tf_op jit(solution)/shard_map/ppermute | solution.py:307
  31.3 1.0 %copy-done.1 = bf16[1536,128]{1,0:T(8,128)(2,1)S(1)} copy-done((bf16[1536,128]{1,0:T(8,128)(2,1)S(1)}, bf16[1536,128]{1,0:T(8,128)(2,1)}, u32[]{:S(2)}) %copy-start.1) | copy-done | bytes 393240
  32.3 0.9 copy-done.2
  33.2 0.7 copy-done.4
  33.9 2.5 %attend.4 = (f32[4,8,512]{2,1,0:T(8,128)S(1)}, f32[4,144,512]{2,1,0:T(8,128)S(1)}) custom-call(s32[1,512]{1,0:T(1,128)S(1)} %copy-done.4, bf16[512,128]{1,0:T(8,128)(2,1)S(1)} %copy-done.2, bf16[512,128]{1,0:T(8,128)(2,1)S(1)} %collective-permute-done.8.refs_2_.refs_1_, bf16[512,128]{1,0:T(8,128)(2,1)S(1)} %collective-permute-done.9.refs_3_.refs_2_, ...), custom_call_target="tpu_custom_call" | custom-call | flops 8000000000 | bytes 4000000 | tf_op jit(solution)/shard_map/attend/pallas_call | solution.py:246
  36.4 1.6 %attend.5 = (f32[4,8,512]{2,1,0:T(8,128)S(1)}, f32[4,144,512]{2,1,0:T(8,128)S(1)}) custom-call(bf16[512,128]{1,0:T(8,128)(2,1)S(1)} %copy-done.3, bf16[512,128]{1,0:T(8,128)(2,1)S(1)} %collective-permute-done.8.refs_2_.refs_1_, bf16[512,128]{1,0:T(8,128)(2,1)S(1)} %collective-permute-done.9.refs_3_.refs_2_, ...), custom_call_target="tpu_custom_call" | custom-call | flops 8000000000 | bytes 4000000 | tf_op jit(solution)/shard_map/attend/pallas_call | solution.py:246
  38.0 2.6 %attend.6 = (f32[4,8,512]{2,1,0:T(8,128)S(1)}, f32[4,144,512]{2,1,0:T(8,128)S(1)}) custom-call(bf16[512,128]{1,0:T(8,128)(2,1)S(1)} %copy-done.3, bf16[512,128]{1,0:T(8,128)(2,1)S(1)} %collective-permute-done.8.refs_2_.refs_1_, bf16[512,128]{1,0:T(8,128)(2,1)S(1)} %collective-permute-done.9.refs_3_.refs_2_, ...), custom_call_target="tpu_custom_call" | custom-call | flops 8000000000 | bytes 4000000 | tf_op jit(solution)/shard_map/attend/pallas_call | solution.py:246
  40.6 1.7 %attend.7 = (bf16[144,512]{1,0:T(8,128)(2,1)S(1)}, bf16[144,512]{1,0:T(8,128)(2,1)S(1)}, bf16[144,512]{1,0:T(8,128)(2,1)S(1)}, bf16[144,512]{1,0:T(8,128)(2,1)S(1)}) custom-call(bf16[512,128]{1,0:T(8,128)(2,1)S(1)} %copy-done.3, bf16[512,128]{1,0:T(8,128)(2,1)S(1)} %collective-permute-done.8.refs_2_.refs_1_, ...), custom_call_target="tpu_custom_call" | custom-call | flops 8000000000 | bytes 4000000 | tf_op jit(solution)/shard_map/attend/pallas_call | solution.py:246
  42.4 4.6 %collective-permute-start.19 = (bf16[144,512]{1,0:T(8,128)(2,1)S(1)}, bf16[144,512]{1,0:T(8,128)(2,1)S(1)}, u32[]{:S(2)}, u32[]{:S(2)}) collective-permute-start(bf16[144,512]{1,0:T(8,128)(2,1)S(1)} %get-tuple-element.30), channel_id=1, source_target_pairs={{64,0},{128,64},{192,128},{0,192},{65,1},{129,65},{193,129},{1,193... | collective-permute-start | bytes 442376 | tf_op jit(solution)/shard_map/ppermute | solution.py:307
  47.0 9.1 %collective-permute-start.20 = (bf16[144,512]{1,0:T(8,128)(2,1)S(1)}, bf16[144,512]{1,0:T(8,128)(2,1)S(1)}, u32[]{:S(2)}, u32[]{:S(2)}) collective-permute-start(bf16[144,512]{1,0:T(8,128)(2,1)S(1)} %get-tuple-element.31), channel_id=1, source_target_pairs={{128,0},{192,64},{0,128},{64,192},{129,1},{193,65},{1,129},{65,193... | collective-permute-start | bytes 442376 | tf_op jit(solution)/shard_map/ppermute | solution.py:307
  56.1 1.9 %collective-permute-start = (f32[8,128]{1,0:T(8,128)S(1)}, f32[8,128]{1,0:T(8,128)S(1)}, u32[]{:S(2)}, u32[]{:S(2)}) collective-permute-start(f32[8,128]{1,0:T(8,128)S(1)} %copy-done.5), channel_id=1, source_target_pairs={{0,1},{1,0},{2,3},{3,2},{4,5},{5,4},{6,7},{7,6},{8,9},{9,8},{10,11... | collective-permute-start | bytes 12296 | tf_op jit(solution)/shard_map/ppermute | solution.py:312
  58.0 1.7 %collective-permute-done = f32[8,128]{1,0:T(8,128)S(1)} collective-permute-done((f32[8,128]{1,0:T(8,128)S(1)}, f32[8,128]{1,0:T(8,128)S(1)}, u32[]{:S(2)}, u32[]{:S(2)}) %collective-permute-start) | collective-permute-done | bytes 4128 | tf_op jit(solution)/shard_map/ppermute | solution.py:312
  59.7 3.3 %collective-permute-start.1 = (f32[8,128]{1,0:T(8,128)S(1)}, f32[8,128]{1,0:T(8,128)S(1)}, u32[]{:S(2)}, u32[]{:S(2)}) collective-permute-start(f32[8,128]{1,0:T(8,128)S(1)} %add.24), channel_id=1, source_target_pairs={{0,2},{1,3},{2,0},{3,1},{4,6},{5,7},{6,4},{7,5},{8,10},{9,11},{10,... | collective-permute-start | bytes 12296 | tf_op jit(solution)/shard_map/ppermute | solution.py:312
  63.0 1.6 %collective-permute-done.1 = f32[8,128]{1,0:T(8,128)S(1)} collective-permute-done((f32[8,128]{1,0:T(8,128)S(1)}, f32[8,128]{1,0:T(8,128)S(1)}, u32[]{:S(2)}, u32[]{:S(2)}) %collective-permute-start.1) | collective-permute-done | bytes 4128 | tf_op jit(solution)/shard_map/ppermute | solution.py:312
  64.6 6.8 %collective-permute-start.2 = (f32[8,128]{1,0:T(8,128)S(1)}, f32[8,128]{1,0:T(8,128)S(1)}, u32[]{:S(2)}, u32[]{:S(2)}) collective-permute-start(f32[8,128]{1,0:T(8,128)S(1)} %add.25), channel_id=1, source_target_pairs={{0,4},{1,5},{2,6},{3,7},{4,0},{5,1},{6,2},{7,3},{8,12},{9,13},{10,... | collective-permute-start | bytes 12296 | tf_op jit(solution)/shard_map/ppermute | solution.py:312
  71.4 1.6 %collective-permute-done.2 = f32[8,128]{1,0:T(8,128)S(1)} collective-permute-done((f32[8,128]{1,0:T(8,128)S(1)}, f32[8,128]{1,0:T(8,128)S(1)}, u32[]{:S(2)}, u32[]{:S(2)}) %collective-permute-start.2) | collective-permute-done | bytes 4128 | tf_op jit(solution)/shard_map/ppermute | solution.py:312
  73.0 1.2 %collective-permute-done.3 = f32[8,128]{1,0:T(8,128)S(1)} collective-permute-done((f32[8,128]{1,0:T(8,128)S(1)}, f32[8,128]{1,0:T(8,128)S(1)}, u32[]{:S(2)}, u32[]{:S(2)}) %collective-permute-start.3) | collective-permute-done | bytes 4128 | tf_op jit(solution)/shard_map/ppermute | solution.py:312
  74.2 3.6 %collective-permute-done.4 = f32[8,128]{1,0:T(8,128)S(1)} collective-permute-done((f32[8,128]{1,0:T(8,128)S(1)}, f32[8,128]{1,0:T(8,128)S(1)}, u32[]{:S(2)}, u32[]{:S(2)}) %collective-permute-start.4) | collective-permute-done | bytes 4128 | tf_op jit(solution)/shard_map/ppermute | solution.py:312
  77.8 2.1 %collective-permute-start.5 = (f32[8,128]{1,0:T(8,128)S(1)}, f32[8,128]{1,0:T(8,128)S(1)}, u32[]{:S(2)}, u32[]{:S(2)}) collective-permute-start(f32[8,128]{1,0:T(8,128)S(1)} %add.28), channel_id=1, source_target_pairs={{0,32},{16,48},{32,0},{48,16},{1,33},{17,49},{33,1},{49,17},{2,34}... | collective-permute-start | bytes 12296 | tf_op jit(solution)/shard_map/ppermute | solution.py:312
  79.8 3.1 %collective-permute-done.5 = f32[8,128]{1,0:T(8,128)S(1)} collective-permute-done((f32[8,128]{1,0:T(8,128)S(1)}, f32[8,128]{1,0:T(8,128)S(1)}, u32[]{:S(2)}, u32[]{:S(2)}) %collective-permute-start.5) | collective-permute-done | bytes 4128 | tf_op jit(solution)/shard_map/ppermute | solution.py:312
  82.9 3.6 %collective-permute-done.6 = f32[8,128]{1,0:T(8,128)S(1)} collective-permute-done((f32[8,128]{1,0:T(8,128)S(1)}, f32[8,128]{1,0:T(8,128)S(1)}, u32[]{:S(2)}, u32[]{:S(2)}) %collective-permute-start.6) | collective-permute-done | bytes 4128 | tf_op jit(solution)/shard_map/ppermute | solution.py:312
  86.5 5.1 %collective-permute-done.7 = f32[8,128]{1,0:T(8,128)S(1)} collective-permute-done((f32[8,128]{1,0:T(8,128)S(1)}, f32[8,128]{1,0:T(8,128)S(1)}, u32[]{:S(2)}, u32[]{:S(2)}) %collective-permute-start.7) | collective-permute-done | bytes 4128 | tf_op jit(solution)/shard_map/ppermute | solution.py:312
  91.7 1.4 %combine.1 = (bf16[120,512]{1,0:T(8,128)(2,1)}, f32[8,128]{1,0:T(8,128)S(1)}) custom-call(s32[4]{0:T(128)S(1)} %copy-done, f32[8,128]{1,0:T(8,128)S(1)} %add.26.dev, f32[8,128]{1,0:T(8,128)S(1)} %add.31.docs, bf16[144,512]{1,0:T(8,128)(2,1)S(1)} %get-tuple-element.28.p0, bf16[144,512]{1,0:T(8,128)(2,1)S(1)} %collective-permute-done.18.p1, ...), custom_call_target="tpu_custom_call" | custom-call | flops 1000000 | bytes 1000000 | tf_op jit(solution)/shard_map/combine/pallas_call | solution.py:291
  93.0 0.6 slice_bitcast_fusion
  (37 shorter events, 1.4 us)
Async XLA Ops:
  8.6 19.9 %collective-permute-start.15 = (bf16[1536,128]{1,0:T(8,128)(2,1)}, bf16[1536,128]{1,0:T(8,128)(2,1)S(1)}, u32[]{:S(2)}, u32[]{:S(2)}) collective-permute-start(bf16[1536,128]{1,0:T(8,128)(2,1)} %get-tuple-element.20.refs_5_), channel_id=1, source_target_pairs={{16,0},{32,16},{48,32},{0,48},{17,1},{33,17},{49,33},{1,49},{18,2}... | collective-permute-start | bytes 1179656 | tf_op jit(solution)/shard_map/ppermute | solution.py:307
  9.1 19.4 %collective-permute-start.13 = (bf16[1536,128]{1,0:T(8,128)(2,1)}, bf16[1536,128]{1,0:T(8,128)(2,1)S(1)}, u32[]{:S(2)}, u32[]{:S(2)}) collective-permute-start(bf16[1536,128]{1,0:T(8,128)(2,1)} %get-tuple-element.20.refs_5_), channel_id=1, source_target_pairs={{48,0},{0,16},{16,32},{32,48},{49,1},{1,17},{17,33},{33,49},{50,2}... | collective-permute-start | bytes 1179656 | tf_op jit(solution)/shard_map/ppermute | solution.py:307
  10.7 18.5 %collective-permute-start.11 = (bf16[1536,128]{1,0:T(8,128)(2,1)}, bf16[1536,128]{1,0:T(8,128)(2,1)S(1)}, u32[]{:S(2)}, u32[]{:S(2)}) collective-permute-start(bf16[1536,128]{1,0:T(8,128)(2,1)} %get-tuple-element.20.refs_5_), channel_id=1, source_target_pairs={{32,0},{48,16},{0,32},{16,48},{33,1},{49,17},{1,33},{17,49},{34,2}... | collective-permute-start | bytes 1179656 | tf_op jit(solution)/shard_map/ppermute | solution.py:307
  14.2 6.7 %collective-permute-start.10 = (bf16[512,128]{1,0:T(8,128)(2,1)}, bf16[512,128]{1,0:T(8,128)(2,1)S(1)}, u32[]{:S(2)}, u32[]{:S(2)}) collective-permute-start(bf16[512,128]{1,0:T(8,128)(2,1)} %get-tuple-element.19.refs_1_.refs_0_), channel_id=1, source_target_pairs={{128,0},{192,64},{0,128},{64,192},{129,1},{193,65},{1,129},{65,193... | collective-permute-start | bytes 393224 | tf_op jit(solution)/shard_map/ppermute | solution.py:307
  14.7 16.6 %collective-permute-start.17 = (bf16[1536,128]{1,0:T(8,128)(2,1)}, bf16[1536,128]{1,0:T(8,128)(2,1)S(1)}, u32[]{:S(2)}, u32[]{:S(2)}) collective-permute-start(bf16[1536,128]{1,0:T(8,128)(2,1)} %get-tuple-element.20.refs_5_), channel_id=1, source_target_pairs={{0,8},{8,0},{1,9},{9,1},{2,10},{10,2},{3,11},{11,3},{4,12},{12,4},... | collective-permute-start | bytes 1179656 | tf_op jit(solution)/shard_map/ppermute | solution.py:312
  20.9 5.2 %collective-permute-start.8 = (bf16[512,128]{1,0:T(8,128)(2,1)}, bf16[512,128]{1,0:T(8,128)(2,1)S(1)}, u32[]{:S(2)}, u32[]{:S(2)}) collective-permute-start(bf16[512,128]{1,0:T(8,128)(2,1)} %get-tuple-element.19.refs_1_.refs_0_), channel_id=1, source_target_pairs={{64,0},{128,64},{192,128},{0,192},{65,1},{129,65},{193,129},{1,193... | collective-permute-start | bytes 393224 | tf_op jit(solution)/shard_map/ppermute | solution.py:307
  26.1 5.2 %collective-permute-start.9 = (bf16[512,128]{1,0:T(8,128)(2,1)}, bf16[512,128]{1,0:T(8,128)(2,1)S(1)}, u32[]{:S(2)}, u32[]{:S(2)}) collective-permute-start(bf16[512,128]{1,0:T(8,128)(2,1)} %get-tuple-element.19.refs_1_.refs_0_), channel_id=1, source_target_pairs={{192,0},{0,64},{64,128},{128,192},{193,1},{1,65},{65,129},{129,193... | collective-permute-start | bytes 393224 | tf_op jit(solution)/shard_map/ppermute | solution.py:307
  28.5 7.9 %collective-permute-start.16 = (bf16[1536,128]{1,0:T(8,128)(2,1)S(1)}, bf16[1536,128]{1,0:T(8,128)(2,1)S(1)}, u32[]{:S(2)}, u32[]{:S(2)}) collective-permute-start(bf16[1536,128]{1,0:T(8,128)(2,1)S(1)} %collective-permute-done.15.refs_4_), channel_id=1, source_target_pairs={{0,8},{8,0},{1,9},{9,1},{2,10},{10,2},{3,11},{11,3},{4,12},{12,4},... | collective-permute-start | bytes 1179656 | tf_op jit(solution)/shard_map/ppermute | solution.py:312
  28.5 9.5 %collective-permute-start.14 = (bf16[1536,128]{1,0:T(8,128)(2,1)S(1)}, bf16[1536,128]{1,0:T(8,128)(2,1)S(1)}, u32[]{:S(2)}, u32[]{:S(2)}) collective-permute-start(bf16[1536,128]{1,0:T(8,128)(2,1)S(1)} %collective-permute-done.13.refs_4_), channel_id=1, source_target_pairs={{0,8},{8,0},{1,9},{9,1},{2,10},{10,2},{3,11},{11,3},{4,12},{12,4},... | collective-permute-start | bytes 1179656 | tf_op jit(solution)/shard_map/ppermute | solution.py:312
  29.2 11.4 %collective-permute-start.12 = (bf16[1536,128]{1,0:T(8,128)(2,1)S(1)}, bf16[1536,128]{1,0:T(8,128)(2,1)S(1)}, u32[]{:S(2)}, u32[]{:S(2)}) collective-permute-start(bf16[1536,128]{1,0:T(8,128)(2,1)S(1)} %collective-permute-done.11.refs_4_), channel_id=1, source_target_pairs={{0,8},{8,0},{1,9},{9,1},{2,10},{10,2},{3,11},{11,3},{4,12},{12,4},... | collective-permute-start | bytes 1179656 | tf_op jit(solution)/shard_map/ppermute | solution.py:312
  31.3 1.0 %copy-start.1 = (bf16[1536,128]{1,0:T(8,128)(2,1)S(1)}, bf16[1536,128]{1,0:T(8,128)(2,1)}, u32[]{:S(2)}) copy-start(bf16[1536,128]{1,0:T(8,128)(2,1)} %get-tuple-element.20.refs_5_) | copy-start | bytes 1179652
  32.3 0.9 copy-start.2
  33.2 0.7 copy-start.4
  33.9 2.5 %copy-start.3 = (bf16[512,128]{1,0:T(8,128)(2,1)S(1)}, bf16[512,128]{1,0:T(8,128)(2,1)}, u32[]{:S(2)}) copy-start(bf16[512,128]{1,0:T(8,128)(2,1)} %get-tuple-element.19.refs_1_.refs_0_) | copy-start | bytes 393220
  40.6 15.5 %copy-start.5 = (f32[8,128]{1,0:T(8,128)S(1)}, f32[8,128]{1,0:T(8,128)}, u32[]{:S(2)}) copy-start(f32[8,128]{1,0:T(8,128)} %get-tuple-element.18) | copy-start | bytes 12292
  40.6 51.1 %copy-start = (s32[4]{0:T(128)S(1)}, s32[4]{0:T(128)}, u32[]{:S(2)}) copy-start(s32[4]{0:T(128)} %lengths.3) | copy-start | bytes 52
  42.3 49.3 %collective-permute-start.18 = (bf16[144,512]{1,0:T(8,128)(2,1)S(1)}, bf16[144,512]{1,0:T(8,128)(2,1)S(1)}, u32[]{:S(2)}, u32[]{:S(2)}) collective-permute-start(bf16[144,512]{1,0:T(8,128)(2,1)S(1)} %get-tuple-element.29), channel_id=1, source_target_pairs={{192,0},{0,64},{64,128},{128,192},{193,1},{1,65},{65,129},{129,193... | collective-permute-start | bytes 442376 | tf_op jit(solution)/shard_map/ppermute | solution.py:307
  42.4 49.3 %collective-permute-start.19 = (bf16[144,512]{1,0:T(8,128)(2,1)S(1)}, bf16[144,512]{1,0:T(8,128)(2,1)S(1)}, u32[]{:S(2)}, u32[]{:S(2)}) collective-permute-start(bf16[144,512]{1,0:T(8,128)(2,1)S(1)} %get-tuple-element.30), channel_id=1, source_target_pairs={{64,0},{128,64},{192,128},{0,192},{65,1},{129,65},{193,129},{1,193... | collective-permute-start | bytes 442376 | tf_op jit(solution)/shard_map/ppermute | solution.py:307
  47.0 44.7 %collective-permute-start.20 = (bf16[144,512]{1,0:T(8,128)(2,1)S(1)}, bf16[144,512]{1,0:T(8,128)(2,1)S(1)}, u32[]{:S(2)}, u32[]{:S(2)}) collective-permute-start(bf16[144,512]{1,0:T(8,128)(2,1)S(1)} %get-tuple-element.31), channel_id=1, source_target_pairs={{128,0},{192,64},{0,128},{64,192},{129,1},{193,65},{1,129},{65,193... | collective-permute-start | bytes 442376 | tf_op jit(solution)/shard_map/ppermute | solution.py:307
  56.1 3.6 %collective-permute-start = (f32[8,128]{1,0:T(8,128)S(1)}, f32[8,128]{1,0:T(8,128)S(1)}, u32[]{:S(2)}, u32[]{:S(2)}) collective-permute-start(f32[8,128]{1,0:T(8,128)S(1)} %copy-done.5), channel_id=1, source_target_pairs={{0,1},{1,0},{2,3},{3,2},{4,5},{5,4},{6,7},{7,6},{8,9},{9,8},{10,11... | collective-permute-start | bytes 12296 | tf_op jit(solution)/shard_map/ppermute | solution.py:312
  59.7 4.8 %collective-permute-start.1 = (f32[8,128]{1,0:T(8,128)S(1)}, f32[8,128]{1,0:T(8,128)S(1)}, u32[]{:S(2)}, u32[]{:S(2)}) collective-permute-start(f32[8,128]{1,0:T(8,128)S(1)} %add.24), channel_id=1, source_target_pairs={{0,2},{1,3},{2,0},{3,1},{4,6},{5,7},{6,4},{7,5},{8,10},{9,11},{10,... | collective-permute-start | bytes 12296 | tf_op jit(solution)/shard_map/ppermute | solution.py:312
  64.6 8.4 %collective-permute-start.2 = (f32[8,128]{1,0:T(8,128)S(1)}, f32[8,128]{1,0:T(8,128)S(1)}, u32[]{:S(2)}, u32[]{:S(2)}) collective-permute-start(f32[8,128]{1,0:T(8,128)S(1)} %add.25), channel_id=1, source_target_pairs={{0,4},{1,5},{2,6},{3,7},{4,0},{5,1},{6,2},{7,3},{8,12},{9,13},{10,... | collective-permute-start | bytes 12296 | tf_op jit(solution)/shard_map/ppermute | solution.py:312
  73.0 1.2 %collective-permute-start.3 = (f32[8,128]{1,0:T(8,128)S(1)}, f32[8,128]{1,0:T(8,128)S(1)}, u32[]{:S(2)}, u32[]{:S(2)}) collective-permute-start(f32[8,128]{1,0:T(8,128)S(1)} %add.26.dev), channel_id=1, source_target_pairs={{0,8},{8,0},{1,9},{9,1},{2,10},{10,2},{3,11},{11,3},{4,12},{12,4},... | collective-permute-start | bytes 12296 | tf_op jit(solution)/shard_map/ppermute | solution.py:312
  74.2 3.6 %collective-permute-start.4 = (f32[8,128]{1,0:T(8,128)S(1)}, f32[8,128]{1,0:T(8,128)S(1)}, u32[]{:S(2)}, u32[]{:S(2)}) collective-permute-start(f32[8,128]{1,0:T(8,128)S(1)} %add.27), channel_id=1, source_target_pairs={{0,16},{16,0},{32,48},{48,32},{1,17},{17,1},{33,49},{49,33},{2,18}... | collective-permute-start | bytes 12296 | tf_op jit(solution)/shard_map/ppermute | solution.py:312
  77.8 5.1 %collective-permute-start.5 = (f32[8,128]{1,0:T(8,128)S(1)}, f32[8,128]{1,0:T(8,128)S(1)}, u32[]{:S(2)}, u32[]{:S(2)}) collective-permute-start(f32[8,128]{1,0:T(8,128)S(1)} %add.28), channel_id=1, source_target_pairs={{0,32},{16,48},{32,0},{48,16},{1,33},{17,49},{33,1},{49,17},{2,34}... | collective-permute-start | bytes 12296 | tf_op jit(solution)/shard_map/ppermute | solution.py:312
  82.9 3.6 %collective-permute-start.6 = (f32[8,128]{1,0:T(8,128)S(1)}, f32[8,128]{1,0:T(8,128)S(1)}, u32[]{:S(2)}, u32[]{:S(2)}) collective-permute-start(f32[8,128]{1,0:T(8,128)S(1)} %add.29), channel_id=1, source_target_pairs={{0,64},{64,0},{128,192},{192,128},{1,65},{65,1},{129,193},{193,129... | collective-permute-start | bytes 12296 | tf_op jit(solution)/shard_map/ppermute | solution.py:312
  86.5 5.1 %collective-permute-start.7 = (f32[8,128]{1,0:T(8,128)S(1)}, f32[8,128]{1,0:T(8,128)S(1)}, u32[]{:S(2)}, u32[]{:S(2)}) collective-permute-start(f32[8,128]{1,0:T(8,128)S(1)} %add.30), channel_id=1, source_target_pairs={{0,128},{64,192},{128,0},{192,64},{1,129},{65,193},{129,1},{193,65... | collective-permute-start | bytes 12296 | tf_op jit(solution)/shard_map/ppermute | solution.py:312

commit v3 on v2

--- a/solution.py
+++ b/solution.py
@@ -18,6 +18,8 @@
 DOCS = 4
 CHUNK = 1024
 NEG = -1e30
+VMEM_PROJECT = 66_000_000
+KV_ROWS = 2 * TOK
 EXP_SCALE = (HEAD_DIM ** -0.5) * math.log2(math.e)
 SEQ = ("x", "y", "c")
 f32, bf16 = jnp.float32, jnp.bfloat16
@@ -117,7 +119,7 @@
         in_specs=[pl.BlockSpec(memory_space=pltpu.SMEM)] + [hbm] * 7,
         out_specs=[vmem] * 4,
         out_shape=[
-            jax.ShapeDtypeStruct((2 * TOK, HEAD_DIM), bf16),
+            jax.ShapeDtypeStruct((KV_ROWS, HEAD_DIM), bf16),
             jax.ShapeDtypeStruct((QROWS, HEAD_DIM), bf16),
             jax.ShapeDtypeStruct((8, ROWS), f32),
             jax.ShapeDtypeStruct((1, QROWS), jnp.int32),
@@ -133,7 +135,7 @@
             pltpu.SemaphoreType.DMA((4, steps)),
             pltpu.SemaphoreType.DMA((3,)),
         ],
-        compiler_params=pltpu.CompilerParams(vmem_limit_bytes=66_400_000),
+        compiler_params=pltpu.CompilerParams(vmem_limit_bytes=VMEM_PROJECT),
         cost_estimate=pl.CostEstimate(flops=5 * 10**9, bytes_accessed=13 * 10**6, transcendentals=0),
         name="project",
     )(lengths, selected, hidden, w_query, w_key, w_value, cached_key, cached_value)
@@ -161,12 +163,30 @@
     acc_s[i] = acc_s[i] * jnp.exp2(old - new) + jnp.dot(values, p, preferred_element_type=f32)
 
 
-def attend_kernel(dy, first, last, *refs):
-    n = 2
+def add_kernel(a, b, out):
+    out[...] = a[...] + b[...]
+
+
+def small(kernel, *args):
+    vmem = pl.BlockSpec(memory_space=pltpu.VMEM)
+    return pl.pallas_call(
+        kernel,
+        in_specs=[vmem] * len(args),
+        out_specs=vmem,
+        out_shape=jax.ShapeDtypeStruct((8, ROWS), f32),
+        compiler_params=pltpu.CompilerParams(vmem_limit_bytes=4 * 2**20),
+        cost_estimate=pl.CostEstimate(flops=10**6, bytes_accessed=10**4, transcendentals=0),
+    )(*args)
+
+
+def attend_kernel(steps, first, last, *refs):
+    n = 2 * len(steps)
     refs = list(refs)
     mask_rows = refs.pop(0) if first else None
+    docs = refs.pop(0) if last else None
     q_in, refs = refs[:4], refs[4:]
     kv_in, refs = refs[:n], refs[n:]
+    own_kv = refs.pop(0) if first else None
     if not first:
         m_in, acc_in, refs = refs[0], refs[1], refs[2:]
     if last:
@@ -177,26 +197,31 @@
     q, kv, s_a, s_b, top_a, top_b, pairs = refs
     for i in range(4):
         q[i] = q_in[i][...]
-    for j in range(n):
-        kv[j] = kv_in[j][...]
+    x, y, c = lax.axis_index("x"), lax.axis_index("y"), lax.axis_index("c")
+    for side in range(2):
+        @pl.when(c == side)
+        def _():
+            for j in range(n):
+                kv[j] = kv_in[j ^ side][...]
+
     if first:
+        kv[n] = own_kv[...]
         m_s[...] = jnp.full_like(m_s, NEG)
         acc_s[...] = jnp.zeros_like(acc_s)
         place = lax.broadcasted_iota(jnp.int32, (TOK, QROWS), 0)
-        s = lax.dot_general(kv[0, :TOK, :], q[0], (((1,), (1,)), ((), ())), preferred_element_type=f32)
+        s = lax.dot_general(kv[n, :TOK, :], q[0], (((1,), (1,)), ((), ())), preferred_element_type=f32)
         s = jnp.where(place <= mask_rows[...], s, NEG)
         s_a[...] = s
         top_a[...] = jnp.max(s.reshape(TOK // 8, 8, QROWS), axis=0)
-        mix_tile(kv, m_s, acc_s, 0, 0, s_a, top_a)
+        mix_tile(kv, m_s, acc_s, 0, n, s_a, top_a)
     else:
         m_s[...] = m_in[...]
         acc_s[...] = acc_in[...]
-    x, y, c = lax.axis_index("x"), lax.axis_index("y"), lax.axis_index("c")
     count = jnp.int32(0)
     for i, dx in enumerate(X_STEPS):
-        for j, dc in enumerate((0, 1)):
+        for j in range(n):
             q_at = ((x + dx) & 3) * 8 + 2 * y + c
-            kv_at = x * 8 + 2 * ((y + dy) & 3) + ((c + dc) & 1)
+            kv_at = (3 - x if j % 2 else x) * 8 + 2 * ((y + steps[j // 2]) & 3) + j % 2
             pairs[count] = i * 8 + j
             count = count + jnp.where(q_at > kv_at, 1, 0)
 
@@ -220,13 +245,14 @@
             mix_tile(kv, m_s, acc_s, *pair(k + 1), s_b, top_b)
 
     if last:
+        pieces = [jnp.concatenate([v] * GROUP, axis=1) for v in split3(docs[6:7, :])]
         for i in range(4):
             total = acc_s[i, HEAD_DIM:HEAD_DIM + 1, :]
             safe = jnp.maximum(total, 1e-30)
             outs[i][:HEAD_DIM, :] = (acc_s[i, :HEAD_DIM, :] * (1.0 / safe)).astype(bf16)
             lse = jnp.where(total > 0.0, m_s[i, 0:1, :] + jnp.log2(safe), NEG)
             outs[i][HEAD_DIM:, :] = jnp.concatenate(
-                split3(lse) + [jnp.zeros((13, QROWS), f32)], axis=0).astype(bf16)
+                split3(lse) + pieces + [jnp.zeros((10, QROWS), f32)], axis=0).astype(bf16)
 
 
 def split3(value):
@@ -235,22 +261,22 @@
     return [high, mid, value - high - mid]
 
 
-def attend(dy, last, qs, kvs, mask_rows, state):
-    first = state is None
-    n = 2
+def attend(steps, qs, kvs, mask_rows=None, own_kv=None, state=None, docs=None):
+    first, last = state is None, docs is not None
+    n = 2 * len(steps)
     vmem = pl.BlockSpec(memory_space=pltpu.VMEM)
-    args = ([mask_rows] if first else []) + list(qs) + list(kvs)
-    args += [] if first else list(state)
+    args = ([mask_rows] if first else []) + ([docs] if last else []) + list(qs) + list(kvs)
+    args += [own_kv] if first else list(state)
     states = [jax.ShapeDtypeStruct((4, 8, QROWS), f32), jax.ShapeDtypeStruct((4, ACC, QROWS), f32)]
     keep = [pltpu.VMEM((4, 8, QROWS), f32), pltpu.VMEM((4, ACC, QROWS), f32)]
     return pl.pallas_call(
-        functools.partial(attend_kernel, dy, first, last),
+        functools.partial(attend_kernel, steps, first, last),
         in_specs=[vmem] * len(args),
         out_specs=[vmem] * (4 if last else 2),
         out_shape=[jax.ShapeDtypeStruct((ACC, QROWS), bf16)] * 4 if last else states,
         scratch_shapes=(keep if last else []) + [
             pltpu.VMEM((4, QROWS, HEAD_DIM), bf16),
-            pltpu.VMEM((n, 2 * TOK, HEAD_DIM), bf16),
+            pltpu.VMEM((n + (1 if first else 0), KV_ROWS, HEAD_DIM), bf16),
             pltpu.VMEM((TOK, QROWS), f32),
             pltpu.VMEM((TOK, QROWS), f32),
             pltpu.VMEM((8, QROWS), f32),
@@ -263,11 +289,11 @@
     )(*args)
 
 
-def combine_kernel(lengths, dev, docs, p0, p1, p2, p3, out, score):
+def combine_kernel(lengths, dev, p0, p1, p2, p3, out, score):
     parts = (p0, p1, p2, p3)
     rows = [p[HEAD_DIM:HEAD_DIM + 16, :].astype(f32) for p in parts]
     lses = [v[0:1] + v[1:2] + v[2:3] for v in rows]
-    total = docs[6:7, :]
+    total = sum([v[3:4, :ROWS] + v[4:5, :ROWS] + v[5:6, :ROWS] for v in rows])
     top = functools.reduce(jnp.maximum, lses)
     weights = [jnp.exp2(v - top) for v in lses]
     scale = 1.0 / sum(weights)
@@ -286,11 +312,11 @@
     score[...] = dev[...] / (mean + 1.0)
 
 
-def combine(lengths, dev, docs, parts):
+def combine(lengths, dev, parts):
     vmem = pl.BlockSpec(memory_space=pltpu.VMEM)
     return pl.pallas_call(
         combine_kernel,
-        in_specs=[pl.BlockSpec(memory_space=pltpu.SMEM)] + [vmem] * 6,
+        in_specs=[pl.BlockSpec(memory_space=pltpu.SMEM)] + [vmem] * 5,
         out_specs=[vmem, vmem],
         out_shape=[
             jax.ShapeDtypeStruct((SEL, GROUP * HEAD_DIM), bf16),
@@ -299,7 +325,7 @@
         compiler_params=pltpu.CompilerParams(vmem_limit_bytes=8 * 2**20),
         cost_estimate=pl.CostEstimate(flops=10**6, bytes_accessed=10**6, transcendentals=0),
         name="combine",
-    )(lengths, dev, docs, *parts)
+    )(lengths, dev, *parts)
 
 
 def fetch(value, axis, step):
@@ -307,6 +333,17 @@
     return lax.ppermute(value, axis, [((i + step) % size, i) for i in range(size)])
 
 
+def between(value, target):
+    moves = []
+    for x in range(4):
+        for y in range(4):
+            for c in range(2):
+                to = target(x, y, c)
+                if to is not None:
+                    moves.append(((x * 4 + y) * 2 + c, (to[0] * 4 + to[1]) * 2 + to[2]))
+    return lax.ppermute(value, SEQ, moves)
+
+
 def exchange(value, axis, bit):
     size = lax.axis_size(axis)
     return lax.ppermute(value, axis, [(i, i ^ bit) for i in range(size)])
@@ -315,26 +352,32 @@
 def program(hidden, w_query, w_key, w_value, cached_key, cached_value, doc_lengths, selected):
     kv, q, dev, mask_rows = project(
         doc_lengths, selected, hidden, w_query, w_key, w_value, cached_key, cached_value)
-    kv_y, kv_c, qs = {0: kv}, {}, [q]
-    for s in (1, 3, 2):
-        kv_y[s] = fetch(kv, "y", s)
+    kept, other, qs = {}, {}, [q]
+    for s in Y_STEPS:
+        kept[s] = between(kv, lambda x, y, c: (3 - x if c else x, (y - s) % 4, c))
+    for s in Y_STEPS:
+        other[s] = exchange(kept[s], "c", 1)
     for s in X_STEPS[1:]:
         qs.append(fetch(q, "x", s))
-    for s in (0, 1, 3, 2):
-        kv_c[s] = exchange(kv_y[s], "c", 1)
     for bit in (1, 2, 4):
-        dev = dev + exchange(dev, "kvh", bit)
-    docs = dev
-    for axis, bit in (("c", 1), ("y", 1), ("y", 2), ("x", 1), ("x", 2)):
-        docs = docs + exchange(docs, axis, bit)
+        dev = small(add_kernel, dev, exchange(dev, "kvh", bit))
+    for axis, bit in (("c", 1), ("y", 1), ("y", 2)):
+        docs = dev if axis == "c" else docs
+        docs = small(add_kernel, docs, exchange(docs, axis, bit))
     state = None
-    for n, s in enumerate(Y_STEPS):
-        state = attend(s, n == len(Y_STEPS) - 1, qs, [kv_y[s], kv_c[s]], mask_rows, state)
+    for n, steps in enumerate(KERNELS):
+        first, last = n == 0, n == len(KERNELS) - 1
+        kvs = sum([[kept[s], other[s]] for s in steps], [])
+        state = attend(steps, qs, kvs, mask_rows if first else None, kv if first else None, state,
+                       docs if last else None)
     mine = [state[0]]
     for n, s in enumerate(X_STEPS[1:]):
         mine.append(fetch(state[n + 1], "x", (4 - s) % 4))
-    attended, score = combine(doc_lengths, dev, docs, mine)
+    attended, score = combine(doc_lengths, dev, mine)
     return attended, score.reshape(-1)[:TOK]
+
+
+KERNELS = ((0,), (1,), (3,), (2,))
 
 
 def solution(mesh):

time: 93.8 us -> 90.7 us (0.967)
  the two profiles are of different devices: /device:TPU:12 before, /device:TPU:1 now
where the time goes in v3:
time: 90.7 us; the launch traced here: 90.4 us
  waiting for transfers between devices  34.5 us (38%)
  starting transfers between devices  32.2 us (36%)
  Pallas kernels  19 us (21%)
  local copies, waits for them, and re-layouts  3.87 us (4%)
    ppermute x6, waiting for transfers between devices, fetch(): lax.ppermute(value, axis, [((i + step) % size, i) for i in range(size)])  28.7 us
    ppermute x10, starting transfers between devices, exchange(): return lax.ppermute(value, axis, [(i, i ^ bit) for i in range(size)])  16.6 us
    ppermute x4, starting transfers between devices, between(): return lax.ppermute(value, SEQ, moves)  11.1 us
    pallas_call x4, Pallas kernels, attend(): pl.pallas_call(functools.partial(attend_kernel, steps, first, last), in_s...  9.66 us
    pallas_call x1, Pallas kernels, project(): pl.pallas_call(project_kernel, in_specs=[pl.BlockSpec(memory_space=pltpu....  7.96 us
    ppermute x10, waiting for transfers between devices, exchange(): return lax.ppermute(value, axis, [(i, i ^ bit) for i in range(size)])  5.84 us
    ppermute x6, starting transfers between devices, fetch(): lax.ppermute(value, axis, [((i + step) % size, i) for i in range(size)])  4.53 us
    unnamed x12, local copies, waits for them, and re-layouts  3.28 us
  transfers between devices with their start and end apart: 20, of which 10 were waited for; matrix products, arithmetic and copies ran while one was open for 0% of the time, Pallas kernels for 8%

profile of v3, /device:TPU:1, one launch (start us, length us, event | category | flops | bytes accessed | tf_op | source)
XLA Modules:
  0.0 90.4 jit_solution(4674337375521576338)
XLA Ops:
  0.6 8.0 %project.1 = (bf16[1536,128]{1,0:T(8,128)(2,1)}, bf16[512,128]{1,0:T(8,128)(2,1)}, f32[8,128]{1,0:T(8,128)}, s32[1,512]{1,0:T(1,128)}) custom-call(s32[4]{0:T(128)} %lengths.3, s32[3840]{0:T(1024)} %selected.1, bf16[768,4096]{1,0:T(8,128)(2,1)} %hidden.1, bf16[4096,512]{1,0:T(8,128)(2,1)} %w_query.1, bf16[4096,128]{1,0:T(8,128)(2,1)} %w_key.1, ...), custom_call_target="tpu_custom_call" | custom-call | flops 5000000000 | bytes 13000000 | tf_op jit(solution)/shard_map/project/pallas_call | solution.py:117
  8.6 5.2 %collective-permute-start.15 = (bf16[1536,128]{1,0:T(8,128)(2,1)}, bf16[1536,128]{1,0:T(8,128)(2,1)S(1)}, u32[]{:S(2)}, u32[]{:S(2)}) collective-permute-start(bf16[1536,128]{1,0:T(8,128)(2,1)} %get-tuple-element.20.refs_7_), channel_id=1, source_target_pairs={{0,0},{8,200},{16,16},{24,216},{32,32},{40,232},{48,48},{56,248},{... | collective-permute-start | bytes 1179656 | tf_op jit(solution)/shard_map/ppermute | solution.py:344
  13.8 1.7 %collective-permute-start = (f32[8,128]{1,0:T(8,128)}, f32[8,128]{1,0:T(8,128)S(1)}, u32[]{:S(2)}, u32[]{:S(2)}) collective-permute-start(f32[8,128]{1,0:T(8,128)} %get-tuple-element.18.a), channel_id=1, source_target_pairs={{0,1},{1,0},{2,3},{3,2},{4,5},{5,4},{6,7},{7,6},{8,9},{9,8},{10,11... | collective-permute-start | bytes 12296 | tf_op jit(solution)/shard_map/ppermute | solution.py:349
  15.5 1.3 %collective-permute-done.b = f32[8,128]{1,0:T(8,128)S(1)} collective-permute-done((f32[8,128]{1,0:T(8,128)}, f32[8,128]{1,0:T(8,128)S(1)}, u32[]{:S(2)}, u32[]{:S(2)}) %collective-permute-start) | collective-permute-done | bytes 4128 | tf_op jit(solution)/shard_map/ppermute | solution.py:349
  16.9 0.7 copy-done
  17.6 2.9 %collective-permute-start.1 = (f32[8,128]{1,0:T(8,128)S(1)}, f32[8,128]{1,0:T(8,128)S(1)}, u32[]{:S(2)}, u32[]{:S(2)}) collective-permute-start(f32[8,128]{1,0:T(8,128)S(1)} %shard_map.95.a), channel_id=1, source_target_pairs={{0,2},{1,3},{2,0},{3,1},{4,6},{5,7},{6,4},{7,5},{8,10},{9,11},{10,... | collective-permute-start | bytes 12296 | tf_op jit(solution)/shard_map/ppermute | solution.py:349
  20.4 1.0 %collective-permute-done.1.b = f32[8,128]{1,0:T(8,128)S(1)} collective-permute-done((f32[8,128]{1,0:T(8,128)S(1)}, f32[8,128]{1,0:T(8,128)S(1)}, u32[]{:S(2)}, u32[]{:S(2)}) %collective-permute-start.1) | collective-permute-done | bytes 4128 | tf_op jit(solution)/shard_map/ppermute | solution.py:349
  21.4 6.1 %collective-permute-start.2 = (f32[8,128]{1,0:T(8,128)S(1)}, f32[8,128]{1,0:T(8,128)S(1)}, u32[]{:S(2)}, u32[]{:S(2)}) collective-permute-start(f32[8,128]{1,0:T(8,128)S(1)} %shard_map.96.a), channel_id=1, source_target_pairs={{0,4},{1,5},{2,6},{3,7},{4,0},{5,1},{6,2},{7,3},{8,12},{9,13},{10,... | collective-permute-start | bytes 12296 | tf_op jit(solution)/shard_map/ppermute | solution.py:349
  27.5 1.0 %collective-permute-done.2.b = f32[8,128]{1,0:T(8,128)S(1)} collective-permute-done((f32[8,128]{1,0:T(8,128)S(1)}, f32[8,128]{1,0:T(8,128)S(1)}, u32[]{:S(2)}, u32[]{:S(2)}) %collective-permute-start.2) | collective-permute-done | bytes 4128 | tf_op jit(solution)/shard_map/ppermute | solution.py:349
  28.6 1.5 %collective-permute-start.3 = (f32[8,128]{1,0:T(8,128)S(1)}, f32[8,128]{1,0:T(8,128)S(1)}, u32[]{:S(2)}, u32[]{:S(2)}) collective-permute-start(f32[8,128]{1,0:T(8,128)S(1)} %shard_map.97.a.dev), channel_id=1, source_target_pairs={{0,8},{8,0},{1,9},{9,1},{2,10},{10,2},{3,11},{11,3},{4,12},{12,4},... | collective-permute-start | bytes 12296 | tf_op jit(solution)/shard_map/ppermute | solution.py:349
  30.0 0.8 collective-permute-done.3.b
  30.9 0.8 collective-permute-start.4
  31.7 1.6 %collective-permute-done.4.b = f32[8,128]{1,0:T(8,128)S(1)} collective-permute-done((f32[8,128]{1,0:T(8,128)S(1)}, f32[8,128]{1,0:T(8,128)S(1)}, u32[]{:S(2)}, u32[]{:S(2)}) %collective-permute-start.4) | collective-permute-done | bytes 4128 | tf_op jit(solution)/shard_map/ppermute | solution.py:349
  33.3 2.4 %collective-permute-start.5 = (f32[8,128]{1,0:T(8,128)S(1)}, f32[8,128]{1,0:T(8,128)S(1)}, u32[]{:S(2)}, u32[]{:S(2)}) collective-permute-start(f32[8,128]{1,0:T(8,128)S(1)} %shard_map.99.a), channel_id=1, source_target_pairs={{0,32},{16,48},{32,0},{48,16},{1,33},{17,49},{33,1},{49,17},{2,34}... | collective-permute-start | bytes 12296 | tf_op jit(solution)/shard_map/ppermute | solution.py:349
  35.8 3.0 %collective-permute-start.13 = (bf16[1536,128]{1,0:T(8,128)(2,1)}, bf16[1536,128]{1,0:T(8,128)(2,1)S(1)}, u32[]{:S(2)}, u32[]{:S(2)}) collective-permute-start(bf16[1536,128]{1,0:T(8,128)(2,1)} %get-tuple-element.20.refs_7_), channel_id=1, source_target_pairs={{0,48},{8,248},{16,0},{24,200},{32,16},{40,216},{48,32},{56,232},{... | collective-permute-start | bytes 1179656 | tf_op jit(solution)/shard_map/ppermute | solution.py:344
  39.3 2.3 %collective-permute-start.9 = (bf16[1536,128]{1,0:T(8,128)(2,1)}, bf16[1536,128]{1,0:T(8,128)(2,1)S(1)}, u32[]{:S(2)}, u32[]{:S(2)}) collective-permute-start(bf16[1536,128]{1,0:T(8,128)(2,1)} %get-tuple-element.20.refs_7_), channel_id=1, source_target_pairs={{0,32},{8,232},{16,48},{24,248},{32,0},{40,200},{48,16},{56,216},{... | collective-permute-start | bytes 1179656 | tf_op jit(solution)/shard_map/ppermute | solution.py:344
  41.6 0.9 %collective-permute-start.6 = (bf16[512,128]{1,0:T(8,128)(2,1)}, bf16[512,128]{1,0:T(8,128)(2,1)S(1)}, u32[]{:S(2)}, u32[]{:S(2)}) collective-permute-start(bf16[512,128]{1,0:T(8,128)(2,1)} %get-tuple-element.19.refs_1_.refs_0_), channel_id=1, source_target_pairs={{64,0},{128,64},{192,128},{0,192},{65,1},{129,65},{193,129},{1,193... | collective-permute-start | bytes 393224 | tf_op jit(solution)/shard_map/ppermute | solution.py:333
  43.0 12.0 %collective-permute-done.6.refs_2_.refs_1_ = bf16[512,128]{1,0:T(8,128)(2,1)S(1)} collective-permute-done((bf16[512,128]{1,0:T(8,128)(2,1)}, bf16[512,128]{1,0:T(8,128)(2,1)S(1)}, u32[]{:S(2)}, u32[]{:S(2)}) %collective-permute-start.6) | collective-permute-done | bytes 131104 | tf_op jit(solution)/shard_map/ppermute | solution.py:333
  55.0 0.9 collective-permute-start.7
  55.9 6.4 %collective-permute-done.7.refs_3_.refs_2_ = bf16[512,128]{1,0:T(8,128)(2,1)S(1)} collective-permute-done((bf16[512,128]{1,0:T(8,128)(2,1)}, bf16[512,128]{1,0:T(8,128)(2,1)S(1)}, u32[]{:S(2)}, u32[]{:S(2)}) %collective-permute-start.7) | collective-permute-done | bytes 131104 | tf_op jit(solution)/shard_map/ppermute | solution.py:333
  63.0 4.8 %collective-permute-done.8.refs_4_.refs_3_ = bf16[512,128]{1,0:T(8,128)(2,1)S(1)} collective-permute-done((bf16[512,128]{1,0:T(8,128)(2,1)}, bf16[512,128]{1,0:T(8,128)(2,1)S(1)}, u32[]{:S(2)}, u32[]{:S(2)}) %collective-permute-start.8) | collective-permute-done | bytes 131104 | tf_op jit(solution)/shard_map/ppermute | solution.py:333
  67.9 1.0 %copy-done.2 = bf16[1536,128]{1,0:T(8,128)(2,1)S(1)} copy-done((bf16[1536,128]{1,0:T(8,128)(2,1)S(1)}, bf16[1536,128]{1,0:T(8,128)(2,1)}, u32[]{:S(2)}) %copy-start.2) | copy-done | bytes 393240
  68.8 0.9 copy-done.3
  69.8 0.7 copy-done.5
  70.4 3.3 %attend.4 = (f32[4,8,512]{2,1,0:T(8,128)S(1)}, f32[4,144,512]{2,1,0:T(8,128)S(1)}) custom-call(s32[1,512]{1,0:T(1,128)S(1)} %copy-done.5, bf16[512,128]{1,0:T(8,128)(2,1)S(1)} %copy-done.3, bf16[512,128]{1,0:T(8,128)(2,1)S(1)} %collective-permute-done.6.refs_2_.refs_1_, bf16[512,128]{1,0:T(8,128)(2,1)S(1)} %collective-permute-done.7.refs_3_.refs_2_, ...), custom_call_target="tpu_custom_call" | custom-call | flops 8000000000 | bytes 4000000 | tf_op jit(solution)/shard_map/attend/pallas_call | solution.py:272
  73.8 2.1 %attend.5 = (f32[4,8,512]{2,1,0:T(8,128)S(1)}, f32[4,144,512]{2,1,0:T(8,128)S(1)}) custom-call(bf16[512,128]{1,0:T(8,128)(2,1)S(1)} %copy-done.4, bf16[512,128]{1,0:T(8,128)(2,1)S(1)} %collective-permute-done.6.refs_2_.refs_1_, bf16[512,128]{1,0:T(8,128)(2,1)S(1)} %collective-permute-done.7.refs_3_.refs_2_, ...), custom_call_target="tpu_custom_call" | custom-call | flops 8000000000 | bytes 4000000 | tf_op jit(solution)/shard_map/attend/pallas_call | solution.py:272
  75.9 2.1 %attend.6 = (f32[4,8,512]{2,1,0:T(8,128)S(1)}, f32[4,144,512]{2,1,0:T(8,128)S(1)}) custom-call(bf16[512,128]{1,0:T(8,128)(2,1)S(1)} %copy-done.4, bf16[512,128]{1,0:T(8,128)(2,1)S(1)} %collective-permute-done.6.refs_2_.refs_1_, bf16[512,128]{1,0:T(8,128)(2,1)S(1)} %collective-permute-done.7.refs_3_.refs_2_, ...), custom_call_target="tpu_custom_call" | custom-call | flops 8000000000 | bytes 4000000 | tf_op jit(solution)/shard_map/attend/pallas_call | solution.py:272
  78.0 2.2 %attend.7 = (bf16[144,512]{1,0:T(8,128)(2,1)S(1)}, bf16[144,512]{1,0:T(8,128)(2,1)S(1)}, bf16[144,512]{1,0:T(8,128)(2,1)S(1)}, bf16[144,512]{1,0:T(8,128)(2,1)S(1)}) custom-call(f32[8,128]{1,0:T(8,128)S(1)} %shard_map.100.refs_0_, bf16[512,128]{1,0:T(8,128)(2,1)S(1)} %copy-done.4, bf16[512,128]{1,0:T(8,128)(2,1)S(1)} %collective-permute-done.6.refs_2_.refs_1_, ...), custom_call_target="tpu_custom_call" | custom-call | flops 8000000000 | bytes 4000000 | tf_op jit(solution)/shard_map/attend/pallas_call | solution.py:272
  80.3 2.7 %collective-permute-start.18 = (bf16[144,512]{1,0:T(8,128)(2,1)S(1)}, bf16[144,512]{1,0:T(8,128)(2,1)S(1)}, u32[]{:S(2)}, u32[]{:S(2)}) collective-permute-start(bf16[144,512]{1,0:T(8,128)(2,1)S(1)} %get-tuple-element.30), channel_id=1, source_target_pairs={{64,0},{128,64},{192,128},{0,192},{65,1},{129,65},{193,129},{1,193... | collective-permute-start | bytes 442376 | tf_op jit(solution)/shard_map/ppermute | solution.py:333
  82.9 3.7 %collective-permute-done.17.p1 = bf16[144,512]{1,0:T(8,128)(2,1)S(1)} collective-permute-done((bf16[144,512]{1,0:T(8,128)(2,1)S(1)}, bf16[144,512]{1,0:T(8,128)(2,1)S(1)}, u32[]{:S(2)}, u32[]{:S(2)}) %collective-permute-start.17) | collective-permute-done | bytes 147488 | tf_op jit(solution)/shard_map/ppermute | solution.py:333
  86.6 1.8 %collective-permute-done.19.p3 = bf16[144,512]{1,0:T(8,128)(2,1)S(1)} collective-permute-done((bf16[144,512]{1,0:T(8,128)(2,1)S(1)}, bf16[144,512]{1,0:T(8,128)(2,1)S(1)}, u32[]{:S(2)}, u32[]{:S(2)}) %collective-permute-start.19) | collective-permute-done | bytes 147488 | tf_op jit(solution)/shard_map/ppermute | solution.py:333
  88.4 1.4 %combine.1 = (bf16[120,512]{1,0:T(8,128)(2,1)}, f32[8,128]{1,0:T(8,128)S(1)}) custom-call(s32[4]{0:T(128)S(1)} %copy-done.1, f32[8,128]{1,0:T(8,128)S(1)} %shard_map.97.a.dev, bf16[144,512]{1,0:T(8,128)(2,1)S(1)} %get-tuple-element.28.p0, bf16[144,512]{1,0:T(8,128)(2,1)S(1)} %collective-permute-done.17.p1, bf16[144,512]{1,0:T(8,128)(2,1)S(1)} %collective-permute-done.18.p2, ...), custom_call_target="tpu_custom_call" | custom-call | flops 1000000 | bytes 1000000 | tf_op jit(solution)/shard_map/combine/pallas_call | solution.py:317
  (33 shorter events, 2.5 us)
Async XLA Ops:
  8.6 33.9 %collective-permute-start.15 = (bf16[1536,128]{1,0:T(8,128)(2,1)}, bf16[1536,128]{1,0:T(8,128)(2,1)S(1)}, u32[]{:S(2)}, u32[]{:S(2)}) collective-permute-start(bf16[1536,128]{1,0:T(8,128)(2,1)} %get-tuple-element.20.refs_7_), channel_id=1, source_target_pairs={{0,0},{8,200},{16,16},{24,216},{32,32},{40,232},{48,48},{56,248},{... | collective-permute-start | bytes 1179656 | tf_op jit(solution)/shard_map/ppermute | solution.py:344
  13.8 3.1 %collective-permute-start = (f32[8,128]{1,0:T(8,128)}, f32[8,128]{1,0:T(8,128)S(1)}, u32[]{:S(2)}, u32[]{:S(2)}) collective-permute-start(f32[8,128]{1,0:T(8,128)} %get-tuple-element.18.a), channel_id=1, source_target_pairs={{0,1},{1,0},{2,3},{3,2},{4,5},{5,4},{6,7},{7,6},{8,9},{9,8},{10,11... | collective-permute-start | bytes 12296 | tf_op jit(solution)/shard_map/ppermute | solution.py:349
  16.9 0.7 copy-start
  17.6 3.9 %collective-permute-start.1 = (f32[8,128]{1,0:T(8,128)S(1)}, f32[8,128]{1,0:T(8,128)S(1)}, u32[]{:S(2)}, u32[]{:S(2)}) collective-permute-start(f32[8,128]{1,0:T(8,128)S(1)} %shard_map.95.a), channel_id=1, source_target_pairs={{0,2},{1,3},{2,0},{3,1},{4,6},{5,7},{6,4},{7,5},{8,10},{9,11},{10,... | collective-permute-start | bytes 12296 | tf_op jit(solution)/shard_map/ppermute | solution.py:349
  21.4 7.1 %collective-permute-start.2 = (f32[8,128]{1,0:T(8,128)S(1)}, f32[8,128]{1,0:T(8,128)S(1)}, u32[]{:S(2)}, u32[]{:S(2)}) collective-permute-start(f32[8,128]{1,0:T(8,128)S(1)} %shard_map.96.a), channel_id=1, source_target_pairs={{0,4},{1,5},{2,6},{3,7},{4,0},{5,1},{6,2},{7,3},{8,12},{9,13},{10,... | collective-permute-start | bytes 12296 | tf_op jit(solution)/shard_map/ppermute | solution.py:349
  28.6 2.3 %collective-permute-start.3 = (f32[8,128]{1,0:T(8,128)S(1)}, f32[8,128]{1,0:T(8,128)S(1)}, u32[]{:S(2)}, u32[]{:S(2)}) collective-permute-start(f32[8,128]{1,0:T(8,128)S(1)} %shard_map.97.a.dev), channel_id=1, source_target_pairs={{0,8},{8,0},{1,9},{9,1},{2,10},{10,2},{3,11},{11,3},{4,12},{12,4},... | collective-permute-start | bytes 12296 | tf_op jit(solution)/shard_map/ppermute | solution.py:349
  30.9 2.5 %collective-permute-start.4 = (f32[8,128]{1,0:T(8,128)S(1)}, f32[8,128]{1,0:T(8,128)S(1)}, u32[]{:S(2)}, u32[]{:S(2)}) collective-permute-start(f32[8,128]{1,0:T(8,128)S(1)} %shard_map.98.a), channel_id=1, source_target_pairs={{0,16},{16,0},{32,48},{48,32},{1,17},{17,1},{33,49},{49,33},{2,18}... | collective-permute-start | bytes 12296 | tf_op jit(solution)/shard_map/ppermute | solution.py:349
  33.3 8.3 %collective-permute-start.5 = (f32[8,128]{1,0:T(8,128)S(1)}, f32[8,128]{1,0:T(8,128)S(1)}, u32[]{:S(2)}, u32[]{:S(2)}) collective-permute-start(f32[8,128]{1,0:T(8,128)S(1)} %shard_map.99.a), channel_id=1, source_target_pairs={{0,32},{16,48},{32,0},{48,16},{1,33},{17,49},{33,1},{49,17},{2,34}... | collective-permute-start | bytes 12296 | tf_op jit(solution)/shard_map/ppermute | solution.py:349
  35.8 26.6 %collective-permute-start.13 = (bf16[1536,128]{1,0:T(8,128)(2,1)}, bf16[1536,128]{1,0:T(8,128)(2,1)S(1)}, u32[]{:S(2)}, u32[]{:S(2)}) collective-permute-start(bf16[1536,128]{1,0:T(8,128)(2,1)} %get-tuple-element.20.refs_7_), channel_id=1, source_target_pairs={{0,48},{8,248},{16,0},{24,200},{32,16},{40,216},{48,32},{56,232},{... | collective-permute-start | bytes 1179656 | tf_op jit(solution)/shard_map/ppermute | solution.py:344
  38.7 23.7 %collective-permute-start.11 = (bf16[1536,128]{1,0:T(8,128)(2,1)}, bf16[1536,128]{1,0:T(8,128)(2,1)S(1)}, u32[]{:S(2)}, u32[]{:S(2)}) collective-permute-start(bf16[1536,128]{1,0:T(8,128)(2,1)} %get-tuple-element.20.refs_7_), channel_id=1, source_target_pairs={{0,16},{8,216},{16,32},{24,232},{32,48},{40,248},{48,0},{56,200},{... | collective-permute-start | bytes 1179656 | tf_op jit(solution)/shard_map/ppermute | solution.py:344
  39.3 23.6 %collective-permute-start.9 = (bf16[1536,128]{1,0:T(8,128)(2,1)}, bf16[1536,128]{1,0:T(8,128)(2,1)S(1)}, u32[]{:S(2)}, u32[]{:S(2)}) collective-permute-start(bf16[1536,128]{1,0:T(8,128)(2,1)} %get-tuple-element.20.refs_7_), channel_id=1, source_target_pairs={{0,32},{8,232},{16,48},{24,248},{32,0},{40,200},{48,16},{56,216},{... | collective-permute-start | bytes 1179656 | tf_op jit(solution)/shard_map/ppermute | solution.py:344
  41.6 13.4 %collective-permute-start.6 = (bf16[512,128]{1,0:T(8,128)(2,1)}, bf16[512,128]{1,0:T(8,128)(2,1)S(1)}, u32[]{:S(2)}, u32[]{:S(2)}) collective-permute-start(bf16[512,128]{1,0:T(8,128)(2,1)} %get-tuple-element.19.refs_1_.refs_0_), channel_id=1, source_target_pairs={{64,0},{128,64},{192,128},{0,192},{65,1},{129,65},{193,129},{1,193... | collective-permute-start | bytes 393224 | tf_op jit(solution)/shard_map/ppermute | solution.py:333
  42.5 25.3 %collective-permute-start.16 = (bf16[1536,128]{1,0:T(8,128)(2,1)S(1)}, bf16[1536,128]{1,0:T(8,128)(2,1)S(1)}, u32[]{:S(2)}, u32[]{:S(2)}) collective-permute-start(bf16[1536,128]{1,0:T(8,128)(2,1)S(1)} %collective-permute-done.15.refs_5_), channel_id=1, source_target_pairs={{0,8},{8,0},{1,9},{9,1},{2,10},{10,2},{3,11},{11,3},{4,12},{12,4},... | collective-permute-start | bytes 1179656 | tf_op jit(solution)/shard_map/ppermute | solution.py:349
  55.0 7.3 %collective-permute-start.7 = (bf16[512,128]{1,0:T(8,128)(2,1)}, bf16[512,128]{1,0:T(8,128)(2,1)S(1)}, u32[]{:S(2)}, u32[]{:S(2)}) collective-permute-start(bf16[512,128]{1,0:T(8,128)(2,1)} %get-tuple-element.19.refs_1_.refs_0_), channel_id=1, source_target_pairs={{192,0},{0,64},{64,128},{128,192},{193,1},{1,65},{65,129},{129,193... | collective-permute-start | bytes 393224 | tf_op jit(solution)/shard_map/ppermute | solution.py:333
  62.3 5.5 %collective-permute-start.8 = (bf16[512,128]{1,0:T(8,128)(2,1)}, bf16[512,128]{1,0:T(8,128)(2,1)S(1)}, u32[]{:S(2)}, u32[]{:S(2)}) collective-permute-start(bf16[512,128]{1,0:T(8,128)(2,1)} %get-tuple-element.19.refs_1_.refs_0_), channel_id=1, source_target_pairs={{128,0},{192,64},{0,128},{64,192},{129,1},{193,65},{1,129},{65,193... | collective-permute-start | bytes 393224 | tf_op jit(solution)/shard_map/ppermute | solution.py:333
  62.3 11.5 %collective-permute-start.14 = (bf16[1536,128]{1,0:T(8,128)(2,1)S(1)}, bf16[1536,128]{1,0:T(8,128)(2,1)S(1)}, u32[]{:S(2)}, u32[]{:S(2)}) collective-permute-start(bf16[1536,128]{1,0:T(8,128)(2,1)S(1)} %collective-permute-done.13.refs_4_), channel_id=1, source_target_pairs={{0,8},{8,0},{1,9},{9,1},{2,10},{10,2},{3,11},{11,3},{4,12},{12,4},... | collective-permute-start | bytes 1179656 | tf_op jit(solution)/shard_map/ppermute | solution.py:349
  62.4 13.4 %collective-permute-start.12 = (bf16[1536,128]{1,0:T(8,128)(2,1)S(1)}, bf16[1536,128]{1,0:T(8,128)(2,1)S(1)}, u32[]{:S(2)}, u32[]{:S(2)}) collective-permute-start(bf16[1536,128]{1,0:T(8,128)(2,1)S(1)} %collective-permute-done.11.refs_4_), channel_id=1, source_target_pairs={{0,8},{8,0},{1,9},{9,1},{2,10},{10,2},{3,11},{11,3},{4,12},{12,4},... | collective-permute-start | bytes 1179656 | tf_op jit(solution)/shard_map/ppermute | solution.py:349
  62.9 15.0 %collective-permute-start.10 = (bf16[1536,128]{1,0:T(8,128)(2,1)S(1)}, bf16[1536,128]{1,0:T(8,128)(2,1)S(1)}, u32[]{:S(2)}, u32[]{:S(2)}) collective-permute-start(bf16[1536,128]{1,0:T(8,128)(2,1)S(1)} %collective-permute-done.9.refs_5_), channel_id=1, source_target_pairs={{0,8},{8,0},{1,9},{9,1},{2,10},{10,2},{3,11},{11,3},{4,12},{12,4},... | collective-permute-start | bytes 1179656 | tf_op jit(solution)/shard_map/ppermute | solution.py:349
  67.8 1.0 %copy-start.2 = (bf16[1536,128]{1,0:T(8,128)(2,1)S(1)}, bf16[1536,128]{1,0:T(8,128)(2,1)}, u32[]{:S(2)}) copy-start(bf16[1536,128]{1,0:T(8,128)(2,1)} %get-tuple-element.20.refs_7_) | copy-start | bytes 1179652
  68.8 0.9 copy-start.3
  69.8 0.7 copy-start.5
  70.4 3.4 %copy-start.4 = (bf16[512,128]{1,0:T(8,128)(2,1)S(1)}, bf16[512,128]{1,0:T(8,128)(2,1)}, u32[]{:S(2)}) copy-start(bf16[512,128]{1,0:T(8,128)(2,1)} %get-tuple-element.19.refs_1_.refs_0_) | copy-start | bytes 393220
  78.0 10.5 %copy-start.1 = (s32[4]{0:T(128)S(1)}, s32[4]{0:T(128)}, u32[]{:S(2)}) copy-start(s32[4]{0:T(128)} %lengths.3) | copy-start | bytes 52
  80.2 6.4 %collective-permute-start.17 = (bf16[144,512]{1,0:T(8,128)(2,1)S(1)}, bf16[144,512]{1,0:T(8,128)(2,1)S(1)}, u32[]{:S(2)}, u32[]{:S(2)}) collective-permute-start(bf16[144,512]{1,0:T(8,128)(2,1)S(1)} %get-tuple-element.29), channel_id=1, source_target_pairs={{192,0},{0,64},{64,128},{128,192},{193,1},{1,65},{65,129},{129,193... | collective-permute-start | bytes 442376 | tf_op jit(solution)/shard_map/ppermute | solution.py:333
  80.3 6.3 %collective-permute-start.18 = (bf16[144,512]{1,0:T(8,128)(2,1)S(1)}, bf16[144,512]{1,0:T(8,128)(2,1)S(1)}, u32[]{:S(2)}, u32[]{:S(2)}) collective-permute-start(bf16[144,512]{1,0:T(8,128)(2,1)S(1)} %get-tuple-element.30), channel_id=1, source_target_pairs={{64,0},{128,64},{192,128},{0,192},{65,1},{129,65},{193,129},{1,193... | collective-permute-start | bytes 442376 | tf_op jit(solution)/shard_map/ppermute | solution.py:333
  82.9 5.5 %collective-permute-start.19 = (bf16[144,512]{1,0:T(8,128)(2,1)S(1)}, bf16[144,512]{1,0:T(8,128)(2,1)S(1)}, u32[]{:S(2)}, u32[]{:S(2)}) collective-permute-start(bf16[144,512]{1,0:T(8,128)(2,1)S(1)} %get-tuple-element.31), channel_id=1, source_target_pairs={{128,0},{192,64},{0,128},{64,192},{129,1},{193,65},{1,129},{65,193... | collective-permute-start | bytes 442376 | tf_op jit(solution)/shard_map/ppermute | solution.py:333
